TPU v7x, 32 devices: a whole 2x2x4 slice. The times are simulated.
32 devices in a mesh: dp: 8 (over z, y), mp: 4 (over x, core).
Axes of the slice: x: 2, y: 2, z: 4, core: 2. Of those that a mesh axis runs over, the one named last changes fastest.
Arguments:
- hidden_in: bfloat16 [16384, 1536], P(('dp', 'mp')), may hold values from -6 to 6
- text_states: bfloat16 [10240, 4096], P('dp'), may hold values from -6 to 6
- modulation: float32 [8, 5, 6144], P('dp'), may hold values from -3 to 3
- image_lengths: int32 [8, 5], P('dp'), may hold values from 1 to 1088, as said below
- text_lengths: int32 [8, 5], P('dp'), may hold values from 32 to 256
- positions: int32 [2, 16384], P(None, 'dp'), may hold values from 0 to 64, as said below
- w_query: bfloat16 [1536, 1536], P(None, 'mp'), may hold values from -0.15625 to 0.15625
- w_key: bfloat16 [1536, 1536], P(None, 'mp'), may hold values from -0.15625 to 0.15625
- w_value: bfloat16 [1536, 1536], P(None, 'mp'), may hold values from -0.15625 to 0.15625
- w_out: bfloat16 [1536, 1536], P('mp'), may hold values from -0.625 to 0.625
- w_text_key: bfloat16 [4096, 1536], P(None, 'mp'), may hold values from -0.09375 to 0.09375
- w_text_value: bfloat16 [4096, 1536], P(None, 'mp'), may hold values from -0.09375 to 0.09375
- w_gate: bfloat16 [1536, 4096], P(None, 'mp'), may hold values from -0.15625 to 0.15625
- w_up: bfloat16 [1536, 4096], P(None, 'mp'), may hold values from -0.15625 to 0.15625
- w_down: bfloat16 [4096, 1536], P('mp'), may hold values from -0.09375 to 0.09375
- attention_gain: float32 [1536], replicated, may hold values from 0.5 to 1.5
- feedforward_gain: float32 [1536], replicated, may hold values from 0.5 to 1.5
- head_gates: float32 [24], replicated, may hold values from 0.3 to 1.2
- out_cotangent: bfloat16 [16384, 1536], P(('dp', 'mp')), may hold values from -6 to 6
Outputs:
- block_out: bfloat16 [16384, 1536], P(('dp', 'mp'))
- input_grad: bfloat16 [16384, 1536], P(('dp', 'mp'))
- modulation_grad: float32 [8, 5, 6144], P('dp')
- grad_w_query: float32 [1536, 1536], P('dp', 'mp')
- grad_w_key: float32 [1536, 1536], P('dp', 'mp')
- grad_w_value: float32 [1536, 1536], P('dp', 'mp')
- grad_w_out: float32 [1536, 1536], P('mp', 'dp')
- grad_w_text_key: float32 [4096, 1536], P('dp', 'mp')
- grad_w_text_value: float32 [4096, 1536], P('dp', 'mp')
- grad_w_gate: float32 [1536, 4096], P('dp', 'mp')
- grad_w_up: float32 [1536, 4096], P('dp', 'mp')
- grad_w_down: float32 [4096, 1536], P('mp', 'dp')
- grad_attention_gain: float32 [1536], replicated
- grad_feedforward_gain: float32 [1536], replicated
- grad_head_gates: float32 [24], replicated
Inputs may be any that keep to these rules, and one draw needn't show every extreme that they name: `image_lengths`: each row holds the 5 segment lengths of one pack, summing to 2048. The first 4 are images in some order: one of r rows and c columns of patches with r c = 32^2 and three with r c = 16^2, each with r in (side/2, side, 2 side) and one nextline token a row, so r (c + 1) tokens; the last segment is a filler. `positions`: row 0 holds each token's row in its segment's grid, row 1 its column; a nextline token takes column c; the filler continues a grid of 32 columns.
All inputs are finite; a program needn't handle non-finite values.
Results may differ from a plain program's by a relative error of at most 0.018.
Values may be sent and summed in bfloat16 or wider, within the bound.
A program may use at most 576 MiB of HBM per device.

v0:
```python
import jax
import jax.numpy as jnp
from jax import lax
from jax.sharding import PartitionSpec as P

D = 1536
H = 24
HD = 64
TXT = 256
IMGS = 5


def rope_tables(places, quarter):
    frequency = 10000.0 ** (-jnp.arange(quarter, dtype=jnp.float32) / quarter)
    angle_row = places[0].astype(jnp.float32)[:, None] * frequency[None, :]
    angle_col = places[1].astype(jnp.float32)[:, None] * frequency[None, :]
    return (
        jnp.cos(angle_row)[:, None, :],
        jnp.sin(angle_row)[:, None, :],
        jnp.cos(angle_col)[:, None, :],
        jnp.sin(angle_col)[:, None, :],
    )


def rotate(values, tables):
    cos_row, sin_row, cos_col, sin_col = tables
    quarter = values.shape[-1] // 4
    part_one = values[..., 0:quarter]
    part_two = values[..., quarter : 2 * quarter]
    part_three = values[..., 2 * quarter : 3 * quarter]
    part_four = values[..., 3 * quarter :]
    return jnp.concatenate(
        [
            part_one * cos_row - part_two * sin_row,
            part_two * cos_row + part_one * sin_row,
            part_three * cos_col - part_four * sin_col,
            part_four * cos_col + part_three * sin_col,
        ],
        -1,
    )


def head_norm(values):
    return values * lax.rsqrt(jnp.mean(values * values, -1, keepdims=True) + 1e-06)


def modulated_norm(row_block, gain_vec, scale_vec):
    return (
        row_block
        * lax.rsqrt(jnp.mean(row_block * row_block, -1, keepdims=True) + 1e-05)
        * gain_vec
        * (1.0 + scale_vec)
    )


def masked_softmax(scores, allowed):
    scores = jnp.where(allowed, scores, -1e30)
    row_peak = jnp.max(scores, -1, keepdims=True)
    exp_scores = jnp.exp(scores - row_peak)
    row_total = jnp.sum(exp_scores, -1, keepdims=True)
    return (exp_scores / row_total, row_peak + jnp.log(row_total))


def on_device(
    hidden_in,
    text_states,
    modulation,
    image_lengths,
    text_lengths,
    positions,
    w_query,
    w_key,
    w_value,
    w_out,
    w_text_key,
    w_text_value,
    w_gate,
    w_up,
    w_down,
    attention_gain,
    feedforward_gain,
    head_gates,
    out_cotangent,
):
    highest = lax.Precision.HIGHEST
    contract_rows = (((0,), (0,)), ((), ()))
    contract_cols = (((1,), (1,)), ((), ()))
    local_rows = hidden_in.shape[0]
    shard_index = lax.axis_index("mp")
    seq_len = local_rows * lax.axis_size("mp")
    local_heads = w_query.shape[1] // HD
    local_width = local_heads * HD
    slot_count = text_states.shape[0]
    image_ids = jnp.arange(IMGS, dtype=jnp.int32)
    token_ids = jnp.arange(seq_len, dtype=jnp.int32)
    image_ends = jnp.cumsum(image_lengths[0])
    image_of = jnp.sum((token_ids[:, None] >= image_ends[None, :]).astype(jnp.int32), 1)
    select_all = (image_of[:, None] == image_ids[None, :]).astype(jnp.float32)
    select_mine = lax.dynamic_slice_in_dim(select_all, shard_index * local_rows, local_rows, 0)
    per_token = jnp.dot(select_mine, modulation[0], precision=highest)
    scale_attn = per_token[:, 0:D]
    gate_attn = per_token[:, D : 2 * D]
    scale_ffn = per_token[:, 2 * D : 3 * D]
    gate_ffn = per_token[:, 3 * D :]
    slot_ids = jnp.arange(slot_count, dtype=jnp.int32)
    slot_image = slot_ids // TXT
    slot_place = slot_ids % TXT
    slot_limit = jnp.sum(
        jnp.where(slot_image[:, None] == image_ids[None, :], text_lengths[0][None, :], 0), 1
    )
    slot_valid = slot_place < slot_limit
    tables = rope_tables(positions, HD // 4)
    scale_qk = HD ** (-0.5)
    hidden_float = hidden_in.astype(jnp.float32)
    normed_one, back_norm_one = jax.vjp(modulated_norm, hidden_float, attention_gain, scale_attn)
    normed_one_low = normed_one.astype(jnp.bfloat16)
    rows_attn = lax.all_gather(normed_one_low, "mp", axis=0, tiled=True)
    w_joint = jnp.concatenate([w_query, w_key, w_value], 1)
    joint = jnp.dot(rows_attn, w_joint, preferred_element_type=jnp.float32)
    query_raw = joint[:, 0:local_width]
    key_raw = joint[:, local_width : 2 * local_width]
    value_low = joint[:, 2 * local_width :].reshape(seq_len, local_heads, HD).astype(jnp.bfloat16)

    def prepare(query_in, key_in):
        return (
            rotate(head_norm(query_in.reshape(seq_len, local_heads, HD)), tables),
            rotate(head_norm(key_in.reshape(seq_len, local_heads, HD)), tables),
        )

    (query_rot, key_rot), back_prepare = jax.vjp(prepare, query_raw, key_raw)
    query_low = query_rot.astype(jnp.bfloat16)
    key_low = key_rot.astype(jnp.bfloat16)
    w_text = jnp.concatenate([w_text_key, w_text_value], 1)
    text_joint = jnp.dot(text_states, w_text, preferred_element_type=jnp.float32)

    def prepare_text(text_key_in):
        return head_norm(text_key_in.reshape(slot_count, local_heads, HD))

    text_key_norm, back_text = jax.vjp(prepare_text, text_joint[:, 0:local_width])
    text_key_low = text_key_norm.astype(jnp.bfloat16)
    text_value_low = (
        text_joint[:, local_width:].reshape(slot_count, local_heads, HD).astype(jnp.bfloat16)
    )
    gate_mine = lax.dynamic_slice_in_dim(head_gates, shard_index * local_heads, local_heads, 0)
    gate_tanh = jnp.tanh(gate_mine)
    block_rows = min(512, seq_len)
    block_count = seq_len // block_rows
    self_parts, cross_parts, self_totals, cross_totals = ([], [], [], [])
    for index in range(block_count):
        lower = index * block_rows
        query_block = query_low[lower : lower + block_rows]
        image_block = image_of[lower : lower + block_rows]
        allow_self = (image_block[:, None] == image_of[None, :])[None]
        allow_cross = ((image_block[:, None] == slot_image[None, :]) & slot_valid[None, :])[None]
        scores = (
            jnp.einsum("qhd,khd->hqk", query_block, key_low, preferred_element_type=jnp.float32)
            * scale_qk
        )
        probs_self, total_self = masked_softmax(scores, allow_self)
        self_parts.append(
            jnp.einsum(
                "hqk,khd->qhd",
                probs_self.astype(jnp.bfloat16),
                value_low,
                preferred_element_type=jnp.float32,
            )
        )
        self_totals.append(total_self)
        scores = (
            jnp.einsum(
                "qhd,khd->hqk", query_block, text_key_low, preferred_element_type=jnp.float32
            )
            * scale_qk
        )
        probs_cross, total_cross = masked_softmax(scores, allow_cross)
        cross_parts.append(
            jnp.einsum(
                "hqk,khd->qhd",
                probs_cross.astype(jnp.bfloat16),
                text_value_low,
                preferred_element_type=jnp.float32,
            )
        )
        cross_totals.append(total_cross)
    out_self = jnp.concatenate(self_parts, 0)
    out_cross = jnp.concatenate(cross_parts, 0)
    mixed_low = (
        (out_self + gate_tanh[None, :, None] * out_cross)
        .astype(jnp.bfloat16)
        .reshape(seq_len, local_width)
    )
    attention_out = lax.psum_scatter(
        jnp.dot(mixed_low, w_out, preferred_element_type=jnp.float32),
        "mp",
        scatter_dimension=0,
        tiled=True,
    )
    tanh_attn = jnp.tanh(gate_attn)
    after_attn = hidden_float + tanh_attn * attention_out
    normed_two, back_norm_two = jax.vjp(modulated_norm, after_attn, feedforward_gain, scale_ffn)
    rows_ffn = lax.all_gather(normed_two.astype(jnp.bfloat16), "mp", axis=0, tiled=True)
    gate_pre = jnp.dot(rows_ffn, w_gate, preferred_element_type=jnp.float32)
    up_pre = jnp.dot(rows_ffn, w_up, preferred_element_type=jnp.float32)
    sigmoid_gate = jax.nn.sigmoid(gate_pre)
    activated = gate_pre * sigmoid_gate
    inner_low = (activated * up_pre).astype(jnp.bfloat16)
    ffn_out = lax.psum_scatter(
        jnp.dot(inner_low, w_down, preferred_element_type=jnp.float32).astype(jnp.bfloat16),
        "mp",
        scatter_dimension=0,
        tiled=True,
    ).astype(jnp.float32)
    tanh_ffn = jnp.tanh(gate_ffn)
    block_out = (after_attn + tanh_ffn * ffn_out).astype(jnp.bfloat16)
    cotangent = out_cotangent.astype(jnp.float32)
    d_ffn_low = (cotangent * tanh_ffn).astype(jnp.bfloat16)
    d_gate_ffn = cotangent * ffn_out * (1.0 - tanh_ffn * tanh_ffn)
    d_ffn_all = lax.all_gather(d_ffn_low, "mp", axis=0, tiled=True)
    grad_down_t = lax.dot_general(
        d_ffn_all, inner_low, contract_rows, preferred_element_type=jnp.float32
    )
    d_inner = lax.dot_general(d_ffn_all, w_down, contract_cols, preferred_element_type=jnp.float32)
    d_gate_low = (d_inner * up_pre * sigmoid_gate * (1.0 + gate_pre * (1.0 - sigmoid_gate))).astype(
        jnp.bfloat16
    )
    d_up_low = (d_inner * activated).astype(jnp.bfloat16)
    grad_gate = lax.dot_general(
        rows_ffn, d_gate_low, contract_rows, preferred_element_type=jnp.float32
    )
    grad_up = lax.dot_general(rows_ffn, d_up_low, contract_rows, preferred_element_type=jnp.float32)
    d_normed_two = lax.psum_scatter(
        lax.dot_general(d_gate_low, w_gate, contract_cols, preferred_element_type=jnp.float32)
        + lax.dot_general(d_up_low, w_up, contract_cols, preferred_element_type=jnp.float32),
        "mp",
        scatter_dimension=0,
        tiled=True,
    )
    d_after_norm, grad_ffn_gain, d_scale_ffn = back_norm_two(d_normed_two)
    d_after = cotangent + d_after_norm
    d_attn_low = (d_after * tanh_attn).astype(jnp.bfloat16)
    d_gate_attn = d_after * attention_out * (1.0 - tanh_attn * tanh_attn)
    d_attn_all = lax.all_gather(d_attn_low, "mp", axis=0, tiled=True)
    grad_out_t = lax.dot_general(
        d_attn_all, mixed_low, contract_rows, preferred_element_type=jnp.float32
    )
    d_mixed = lax.dot_general(
        d_attn_all, w_out, contract_cols, preferred_element_type=jnp.float32
    ).reshape(seq_len, local_heads, HD)
    grad_heads = jnp.sum(d_mixed * out_cross, (0, 2)) * (1.0 - gate_tanh * gate_tanh)
    d_self_low = d_mixed.astype(jnp.bfloat16)
    d_cross_low = (gate_tanh[None, :, None] * d_mixed).astype(jnp.bfloat16)
    d_key_acc = jnp.zeros((seq_len, local_heads, HD), jnp.float32)
    d_value_acc = jnp.zeros((seq_len, local_heads, HD), jnp.float32)
    d_text_key_acc = jnp.zeros((slot_count, local_heads, HD), jnp.float32)
    d_text_value_acc = jnp.zeros((slot_count, local_heads, HD), jnp.float32)
    d_query_parts = []
    for index in range(block_count):
        lower = index * block_rows
        query_block = query_low[lower : lower + block_rows]
        image_block = image_of[lower : lower + block_rows]
        allow_self = (image_block[:, None] == image_of[None, :])[None]
        allow_cross = ((image_block[:, None] == slot_image[None, :]) & slot_valid[None, :])[None]
        d_self_block = d_self_low[lower : lower + block_rows]
        d_cross_block = d_cross_low[lower : lower + block_rows]
        scores = (
            jnp.einsum("qhd,khd->hqk", query_block, key_low, preferred_element_type=jnp.float32)
            * scale_qk
        )
        probs_self = jnp.exp(jnp.where(allow_self, scores, -1e30) - self_totals[index])
        d_probs = jnp.einsum(
            "qhd,khd->hqk", d_self_block, value_low, preferred_element_type=jnp.float32
        )
        row_delta = jnp.sum(probs_self * d_probs, -1, keepdims=True)
        d_scores = (probs_self * (d_probs - row_delta)).astype(jnp.bfloat16)
        d_query_block = (
            jnp.einsum("hqk,khd->qhd", d_scores, key_low, preferred_element_type=jnp.float32)
            * scale_qk
        )
        d_key_acc = (
            d_key_acc
            + jnp.einsum("hqk,qhd->khd", d_scores, query_block, preferred_element_type=jnp.float32)
            * scale_qk
        )
        d_value_acc = d_value_acc + jnp.einsum(
            "hqk,qhd->khd",
            probs_self.astype(jnp.bfloat16),
            d_self_block,
            preferred_element_type=jnp.float32,
        )
        scores = (
            jnp.einsum(
                "qhd,khd->hqk", query_block, text_key_low, preferred_element_type=jnp.float32
            )
            * scale_qk
        )
        probs_cross = jnp.exp(jnp.where(allow_cross, scores, -1e30) - cross_totals[index])
        d_probs = jnp.einsum(
            "qhd,khd->hqk", d_cross_block, text_value_low, preferred_element_type=jnp.float32
        )
        row_delta = jnp.sum(probs_cross * d_probs, -1, keepdims=True)
        d_scores = (probs_cross * (d_probs - row_delta)).astype(jnp.bfloat16)
        d_query_block = (
            d_query_block
            + jnp.einsum("hqk,khd->qhd", d_scores, text_key_low, preferred_element_type=jnp.float32)
            * scale_qk
        )
        d_text_key_acc = (
            d_text_key_acc
            + jnp.einsum("hqk,qhd->khd", d_scores, query_block, preferred_element_type=jnp.float32)
            * scale_qk
        )
        d_text_value_acc = d_text_value_acc + jnp.einsum(
            "hqk,qhd->khd",
            probs_cross.astype(jnp.bfloat16),
            d_cross_block,
            preferred_element_type=jnp.float32,
        )
        d_query_parts.append(d_query_block)
    d_query_raw, d_key_raw = back_prepare((jnp.concatenate(d_query_parts, 0), d_key_acc))
    (d_text_key_raw,) = back_text(d_text_key_acc)
    d_joint_low = jnp.concatenate(
        [d_query_raw, d_key_raw, d_value_acc.reshape(seq_len, local_width)], 1
    ).astype(jnp.bfloat16)
    d_text_low = jnp.concatenate(
        [d_text_key_raw, d_text_value_acc.reshape(slot_count, local_width)], 1
    ).astype(jnp.bfloat16)
    grad_joint = lax.dot_general(
        rows_attn, d_joint_low, contract_rows, preferred_element_type=jnp.float32
    )
    grad_text = lax.dot_general(
        text_states, d_text_low, contract_rows, preferred_element_type=jnp.float32
    )
    d_normed_one = lax.psum_scatter(
        lax.dot_general(d_joint_low, w_joint, contract_cols, preferred_element_type=jnp.float32),
        "mp",
        scatter_dimension=0,
        tiled=True,
    )
    d_hidden_norm, grad_attn_gain, d_scale_attn = back_norm_one(d_normed_one)
    input_grad = (d_after + d_hidden_norm).astype(jnp.bfloat16)
    d_per_token = jnp.concatenate([d_scale_attn, d_gate_attn, d_scale_ffn, d_gate_ffn], 1)
    mod_partial = lax.dot_general(select_mine, d_per_token, contract_rows, precision=highest)
    modulation_grad = lax.psum(mod_partial.astype(jnp.bfloat16), "mp").astype(jnp.float32)[None]
    heads_full = lax.dynamic_update_slice(
        jnp.zeros((H,), jnp.float32), grad_heads, (shard_index * local_heads,)
    )
    gain_attn_sum, gain_ffn_sum, heads_sum = lax.psum(
        (grad_attn_gain, grad_ffn_gain, heads_full), ("dp", "mp")
    )
    grad_query = grad_joint[:, 0:local_width]
    grad_key = grad_joint[:, local_width : 2 * local_width]
    grad_value = grad_joint[:, 2 * local_width :]
    grad_text_key = grad_text[:, 0:local_width]
    grad_text_value = grad_text[:, local_width:]
    reduced = (
        lax.psum_scatter(
            grad_query.astype(jnp.bfloat16), "dp", scatter_dimension=0, tiled=True
        ).astype(jnp.float32),
        lax.psum_scatter(
            grad_key.astype(jnp.bfloat16), "dp", scatter_dimension=0, tiled=True
        ).astype(jnp.float32),
        lax.psum_scatter(
            grad_value.astype(jnp.bfloat16), "dp", scatter_dimension=0, tiled=True
        ).astype(jnp.float32),
        lax.psum_scatter(
            grad_out_t.astype(jnp.bfloat16), "dp", scatter_dimension=0, tiled=True
        ).astype(jnp.float32),
        lax.psum_scatter(
            grad_text_key.astype(jnp.bfloat16), "dp", scatter_dimension=0, tiled=True
        ).astype(jnp.float32),
        lax.psum_scatter(
            grad_text_value.astype(jnp.bfloat16), "dp", scatter_dimension=0, tiled=True
        ).astype(jnp.float32),
        lax.psum_scatter(
            grad_gate.astype(jnp.bfloat16), "dp", scatter_dimension=0, tiled=True
        ).astype(jnp.float32),
        lax.psum_scatter(
            grad_up.astype(jnp.bfloat16), "dp", scatter_dimension=0, tiled=True
        ).astype(jnp.float32),
        lax.psum_scatter(
            grad_down_t.astype(jnp.bfloat16), "dp", scatter_dimension=0, tiled=True
        ).astype(jnp.float32),
    )
    return (
        block_out,
        input_grad,
        modulation_grad,
        reduced[0],
        reduced[1],
        reduced[2],
        reduced[3].T,
        reduced[4],
        reduced[5],
        reduced[6],
        reduced[7],
        reduced[8].T,
        gain_attn_sum,
        gain_ffn_sum,
        heads_sum,
    )


def solution(mesh):
    placed = (
        P(("dp", "mp"), None),
        P("dp", None),
        P("dp", None, None),
        P("dp", None),
        P("dp", None),
        P(None, "dp"),
        P(None, "mp"),
        P(None, "mp"),
        P(None, "mp"),
        P("mp", None),
        P(None, "mp"),
        P(None, "mp"),
        P(None, "mp"),
        P(None, "mp"),
        P("mp", None),
        P(),
        P(),
        P(),
        P(("dp", "mp"), None),
    )
    return jax.shard_map(
        on_device,
        mesh=mesh,
        in_specs=placed,
        out_specs=(
            P(("dp", "mp"), None),
            P(("dp", "mp"), None),
            P("dp", None, None),
            P("dp", "mp"),
            P("dp", "mp"),
            P("dp", "mp"),
            P("mp", "dp"),
            P("dp", "mp"),
            P("dp", "mp"),
            P("dp", "mp"),
            P("dp", "mp"),
            P("mp", "dp"),
            P(),
            P(),
            P(),
        ),
        check_vma=False,
    )
```

profile of v0, /device:TPU:0, one launch (start us, length us, event | category | flops | bytes accessed | tf_op | source)
XLA Modules:
  0.0 1827.7 jit_solution(6978031756730541136)
XLA Ops:
  24.6 16.1 fusion.68
  60.5 13.0 all-gather.5.cloned.1.call-done
  322.6 99.7 %reduce-scatter.14.cloned.1.call-done = f32[512,1536]{1,0:T(8,128)} async-done(((f32[2048,1536]{1,0:T(8,128)}), f32[512,1536]{1,0:T(8,128)}) %reduce-scatter.14.cloned.1.call-update) | async-done | bytes 3145744 | tf_op jit(solution)/shard_map/reduce_scatter | solution.py:192
  434.3 45.9 %all-gather.7.cloned.1.call-done = bf16[2048,1536]{1,0:T(8,128)(2,1)} async-done(((bf16[512,1536]{1,0:T(8,128)(2,1)}), bf16[2048,1536]{1,0:T(8,128)(2,1)}) %all-gather.7.cloned.1.call-update) | async-done | bytes 6291472 | tf_op jit(solution)/shard_map/all_gather | solution.py:201
  501.0 27.6 %all-gather.9.cloned.1.call-done = bf16[2048,1536]{1,0:T(8,128)(2,1)} async-done(((bf16[512,1536]{1,0:T(8,128)(2,1)}), bf16[2048,1536]{1,0:T(8,128)(2,1)}) %all-gather.9.cloned.1.call-update) | async-done | bytes 6291472 | tf_op jit(solution)/shard_map/all_gather | solution.py:218
  528.6 18.9 %multiply_convert_fusion.8 = (bf16[2048,1024]{1,0:T(8,128)(2,1)}, bf16[2048,1024]{1,0:T(8,128)(2,1)}, bf16[2048,1024]{1,0:T(8,128)(2,1)}) fusion(f32[2048,1024]{1,0:T(8,128)} %fusion.203, f32[2048,1024]{1,0:T(8,128)} %fusion.204, bf16[2048,1536]{1,0:T(8,128)(2,1)} %all-gather.9.cloned.1.call-done, bf16[1024,1536]{1,0:T(8,128)(2,1)S(1)} %copy-done), kind=kOutput, calls=%fused_computation.85 | convolution fusion | flops 6473908224 | bytes 38797312 | tf_op jit(solution)/shard_map/dot_general | solution.py:222
  559.2 13.1 convolution_add_fusion
  584.0 88.1 %reduce-scatter.18.cloned.1.call-done = f32[512,1536]{1,0:T(8,128)} async-done(((f32[2048,1536]{1,0:T(8,128)}), f32[512,1536]{1,0:T(8,128)}) %reduce-scatter.18.cloned.1.call-update) | async-done | bytes 3145744 | tf_op jit(solution)/shard_map/reduce_scatter | solution.py:231
  678.5 54.9 %reduce-scatter.16.cloned.1.call-done = bf16[512,1536]{1,0:T(8,128)(2,1)} async-done(((bf16[2048,1536]{1,0:T(8,128)(2,1)}), bf16[512,1536]{1,0:T(8,128)(2,1)}) %reduce-scatter.16.cloned.1.call-update) | async-done | bytes 1572880 | tf_op jit(solution)/shard_map/reduce_scatter | solution.py:207
  805.1 21.1 %multiply_reduce_fusion.1 = (f32[6,512]{1,0:T(8,128)}, f32[6,512,2048]{2,1,0:T(8,128)}) fusion(f32[6,512,2048]{2,1,0:T(8,128)} %get-tuple-element.122, f32[6,512]{1,0:T(8,128)S(1)} %log_add_fusion.3, bf16[2048,6,64]{0,2,1:T(8,128)(2,1)S(1)} %bitcast.169, bf16[2048,6,64]{0,2,1:T(8,128)(2,1)S(1)} %convert_element_type.233), kind=kOutput, calls=%fused_computation.4 | convolution fusion | flops 824177664 | bytes 52326400 | tf_op jit(solution)/shard_map/qhd,khd->hqk/dot_general | solution.py:270
  826.2 22.5 %multiply_convert_fusion.1 = bf16[6,512,2048]{2,1,0:T(8,128)(2,1)} fusion(f32[6,512,2048]{2,1,0:T(8,128)} %get-tuple-element.136, f32[6,512,2048]{2,1,0:T(8,128)} %get-tuple-element.122, f32[6,512]{1,0:T(8,128)} %get-tuple-element.135, f32[6,512]{1,0:T(8,128)} %copy-done.113), kind=kLoop, calls=%fused_computation.3 | loop fusion | flops 25165824 | bytes 62939136 | tf_op jit(solution)/shard_map/convert_element_type | solution.py:274
  866.8 14.2 fusion.16
  881.0 17.3 multiply_reduce_fusion.2
  898.3 22.6 %multiply_convert_fusion.2 = bf16[6,512,2048]{2,1,0:T(8,128)(2,1)} fusion(f32[6,512,2048]{2,1,0:T(8,128)} %get-tuple-element.140, f32[6,512,2048]{2,1,0:T(8,128)} %get-tuple-element.124, f32[6,512]{1,0:T(8,128)} %get-tuple-element.139, f32[6,512]{1,0:T(8,128)} %log_add_fusion.5), kind=kLoop, calls=%fused_computation.6 | loop fusion | flops 25165824 | bytes 62939136 | tf_op jit(solution)/shard_map/convert_element_type | solution.py:274
  939.1 16.6 multiply_reduce_fusion.3
  955.7 22.5 %multiply_convert_fusion.3 = bf16[6,512,2048]{2,1,0:T(8,128)(2,1)} fusion(f32[6,512,2048]{2,1,0:T(8,128)} %get-tuple-element.138, f32[6,512,2048]{2,1,0:T(8,128)} %get-tuple-element.126, f32[6,512]{1,0:T(8,128)} %get-tuple-element.137, f32[6,512]{1,0:T(8,128)} %log_add_fusion.7), kind=kLoop, calls=%fused_computation.9 | loop fusion | flops 25165824 | bytes 62939136 | tf_op jit(solution)/shard_map/convert_element_type | solution.py:274
  1007.8 13.3 multiply_reduce_fusion.5
  1021.1 12.6 multiply_reduce_fusion.6
  1042.9 16.5 multiply_reduce_fusion
  1059.4 21.8 %multiply_convert_fusion = bf16[6,512,2048]{2,1,0:T(8,128)(2,1)} fusion(f32[6,512,2048]{2,1,0:T(8,128)} %get-tuple-element.142, f32[6,512,2048]{2,1,0:T(8,128)} %get-tuple-element.120, f32[6,512]{1,0:T(8,128)} %get-tuple-element.141, f32[6,512]{1,0:T(8,128)} %log_add_fusion.1), kind=kLoop, calls=%fused_computation | loop fusion | flops 25165824 | bytes 62939136 | tf_op jit(solution)/shard_map/convert_element_type | solution.py:274
  1115.5 15.0 multiply_convert_fusion.6
  1175.6 12.2 fusion.14
  1187.8 12.1 fusion.12
  1199.9 15.3 add_convert_fusion
  1302.5 13.4 fusion.109
  1324.2 36.9 %reduce-scatter.24.cloned.1.call-done = bf16[192,384]{1,0:T(8,128)(2,1)} async-done(((bf16[1536,384]{1,0:T(8,128)(2,1)}), bf16[192,384]{1,0:T(8,128)(2,1)}) %reduce-scatter.24.cloned.1.call-update) | async-done | bytes 147472 | tf_op jit(solution)/shard_map/reduce_scatter | solution.py:359
  1362.7 66.1 %reduce-scatter.26.cloned.1.call-done = bf16[192,384]{1,0:T(8,128)(2,1)} async-done(((bf16[1536,384]{1,0:T(8,128)(2,1)}), bf16[192,384]{1,0:T(8,128)(2,1)}) %reduce-scatter.26.cloned.1.call-update) | async-done | bytes 147472 | tf_op jit(solution)/shard_map/reduce_scatter | solution.py:362
  1430.5 65.4 %reduce-scatter.28.cloned.1.call-done = bf16[192,384]{1,0:T(8,128)(2,1)} async-done(((bf16[1536,384]{1,0:T(8,128)(2,1)}), bf16[192,384]{1,0:T(8,128)(2,1)}) %reduce-scatter.28.cloned.1.call-update) | async-done | bytes 147472 | tf_op jit(solution)/shard_map/reduce_scatter | solution.py:365
  1497.5 75.5 %reduce-scatter.30.cloned.1.call-done = bf16[512,384]{0,1:T(8,128)(2,1)} async-done(((bf16[4096,384]{0,1:T(8,128)(2,1)}), bf16[512,384]{0,1:T(8,128)(2,1)}) %reduce-scatter.30.cloned.1.call-update) | async-done | bytes 393232 | tf_op jit(solution)/shard_map/reduce_scatter | solution.py:368
  1575.0 75.5 %reduce-scatter.32.cloned.1.call-done = bf16[512,384]{0,1:T(8,128)(2,1)} async-done(((bf16[4096,384]{0,1:T(8,128)(2,1)}), bf16[512,384]{0,1:T(8,128)(2,1)}) %reduce-scatter.32.cloned.1.call-update) | async-done | bytes 393232 | tf_op jit(solution)/shard_map/reduce_scatter | solution.py:371
  1652.5 99.4 %reduce-scatter.20.cloned.1.call-done = f32[512,1536]{1,0:T(8,128)} async-done(((f32[2048,1536]{1,0:T(8,128)}), f32[512,1536]{1,0:T(8,128)}) %reduce-scatter.20.cloned.1.call-update) | async-done | bytes 3145744 | tf_op jit(solution)/shard_map/reduce_scatter | solution.py:333
  1773.8 40.7 %all-reduce.8 = (f32[1536]{0:T(1024)}, f32[1536]{0:T(1024)}, f32[24]{0:T(128)}) all-reduce(f32[1536]{0:T(1024)S(1)} %get-tuple-element.47, f32[1536]{0:T(1024)S(1)} %copy-done.159, f32[24]{0:T(128)S(1)} %multiply_dynamic-update-slice_fusion), channel_id=1, replica_groups=mesh['dp'=8,'mp'=4] {'dp','mp'}, use_global_device_ids=true, to_apply=%region_52.53 | all-reduce | flops 3096 | bytes 24768 | tf_op jit(solution)/shard_map/psum | solution.py:347
  (595 shorter events, 706.0 us)
Async XLA Ops:
  7.2 521.4 %copy-start = (bf16[1024,1536]{1,0:T(8,128)(2,1)S(1)}, bf16[1024,1536]{1,0:T(8,128)(2,1)}, u32[]{:S(2)}) copy-start(bf16[1024,1536]{1,0:T(8,128)(2,1)} %param.33) | copy-start | bytes 9437188
  7.2 66.3 %all-gather.5.cloned.1.call-start = ((), (), s32[]{:S(2)}) async-start(), calls=%async_computation.13 | async-start | bytes 7864320 | tf_op jit(solution)/shard_map/all_gather | solution.py:117
  24.3 398.1 %reduce-scatter.14.cloned.1.call-start = ((), (), s32[]{:S(2)}) async-start(), calls=%async_computation.14 | async-start | bytes 15728640 | tf_op jit(solution)/shard_map/reduce_scatter | solution.py:192
  53.1 39.8 %copy-start.42 = (f32[2048,16]{0,1:T(8,128)}, f32[2048,16]{0,1:T(8,128)S(1)}, u32[]{:S(2)}) copy-start(f32[2048,16]{0,1:T(8,128)S(1)} %get-tuple-element.104) | copy-start | bytes 393220
  53.1 39.8 %copy-start.44 = (f32[2048,16]{0,1:T(8,128)}, f32[2048,16]{0,1:T(8,128)S(1)}, u32[]{:S(2)}) copy-start(f32[2048,16]{0,1:T(8,128)S(1)} %get-tuple-element.105) | copy-start | bytes 393220
  53.1 39.8 %copy-start.46 = (f32[2048,16]{0,1:T(8,128)}, f32[2048,16]{0,1:T(8,128)S(1)}, u32[]{:S(2)}) copy-start(f32[2048,16]{0,1:T(8,128)S(1)} %get-tuple-element.117) | copy-start | bytes 393220
  93.6 188.6 %copy-start.21 = (bf16[2048,6,64]{0,2,1:T(8,128)(2,1)}, bf16[2048,6,64]{0,2,1:T(8,128)(2,1)S(1)}, u32[]{:S(2)}) copy-start(bf16[2048,6,64]{0,2,1:T(8,128)(2,1)S(1)} %pad_maximum_fusion.5) | copy-start | bytes 4718596
  208.4 31.7 %copy-start.134 = (f32[6,512]{1,0:T(8,128)}, f32[6,512]{1,0:T(8,128)S(1)}, u32[]{:S(2)}) copy-start(f32[6,512]{1,0:T(8,128)S(1)} %get-tuple-element.121) | copy-start | bytes 36868
  322.6 103.9 %copy-start.125 = (f32[1536]{0:T(1024)S(1)}, f32[1536]{0:T(1024)}, u32[]{:S(2)}) copy-start(f32[1536]{0:T(1024)} %param.35) | copy-start | bytes 18436
  322.6 157.6 %all-gather.7.cloned.1.call-start = ((), (), s32[]{:S(2)}) async-start(), calls=%async_computation.15 | async-start | bytes 7864320 | tf_op jit(solution)/shard_map/all_gather | solution.py:201
  433.7 94.9 %all-gather.9.cloned.1.call-start = ((), (), s32[]{:S(2)}) async-start(), calls=%async_computation.17 | async-start | bytes 7864320 | tf_op jit(solution)/shard_map/all_gather | solution.py:218
  434.3 237.8 %reduce-scatter.18.cloned.1.call-start = ((), (), s32[]{:S(2)}) async-start(), calls=%async_computation.18 | async-start | bytes 15728640 | tf_op jit(solution)/shard_map/reduce_scatter | solution.py:231
  572.4 161.0 %reduce-scatter.16.cloned.1.call-start = ((), (), s32[]{:S(2)}) async-start(), calls=%async_computation.16 | async-start | bytes 7864320 | tf_op jit(solution)/shard_map/reduce_scatter | solution.py:207
  583.9 88.2 %copy-start.16 = (f32[512,1536]{1,0:T(8,128)S(1)}, f32[512,1536]{1,0:T(8,128)}, u32[]{:S(2)}) copy-start(f32[512,1536]{1,0:T(8,128)} %copy-done.15) | copy-start | bytes 9437188
  583.9 211.8 %all-gather.11.cloned.1.call-start = ((), (), s32[]{:S(2)}) async-start(), calls=%async_computation.19 | async-start | bytes 7864320 | tf_op jit(solution)/shard_map/all_gather | solution.py:242
  749.2 566.7 %reduce-scatter.36.cloned.1.call-start = ((), (), s32[]{:S(2)}) async-start(), calls=%async_computation.28 | async-start | bytes 3538944 | tf_op jit(solution)/shard_map/reduce_scatter | solution.py:377
  760.7 557.2 %reduce-scatter.34.cloned.1.call-start = ((), (), s32[]{:S(2)}) async-start(), calls=%async_computation.27 | async-start | bytes 3538944 | tf_op jit(solution)/shard_map/reduce_scatter | solution.py:374
  772.2 547.8 %reduce-scatter.38.cloned.1.call-start = ((), (), s32[]{:S(2)}) async-start(), calls=%async_computation.29 | async-start | bytes 3538944 | tf_op jit(solution)/shard_map/reduce_scatter | solution.py:380
  774.7 221.9 %copy-start.109 = (f32[6,512]{1,0:T(8,128)}, f32[6,512]{1,0:T(8,128)S(1)}, u32[]{:S(2)}) copy-start(f32[6,512]{1,0:T(8,128)S(1)} %log_add_fusion) | copy-start | bytes 36868
  775.3 28.6 %copy-start.113 = (f32[6,512]{1,0:T(8,128)}, f32[6,512]{1,0:T(8,128)S(1)}, u32[]{:S(2)}) copy-start(f32[6,512]{1,0:T(8,128)S(1)} %log_add_fusion.3) | copy-start | bytes 36868
  787.9 534.7 %reduce-scatter.22.cloned.1.call-start = ((), (), s32[]{:S(2)}) async-start(), calls=%async_computation.21 | async-start | bytes 1327104 | tf_op jit(solution)/shard_map/reduce_scatter | solution.py:356
  1099.9 43.2 %copy-start.3 = (bf16[6,512,1280]{2,1,0:T(8,128)(2,1)}, bf16[6,512,1280]{2,1,0:T(8,128)(2,1)S(1)}, u32[]{:S(2)}) copy-start(bf16[6,512,1280]{2,1,0:T(8,128)(2,1)S(1)} %multiply_convert_fusion.4) | copy-start | bytes 23592964
  1229.1 132.0 %reduce-scatter.24.cloned.1.call-start = ((), (), s32[]{:S(2)}) async-start(), calls=%async_computation.22 | async-start | bytes 1327104 | tf_op jit(solution)/shard_map/reduce_scatter | solution.py:359
  1229.7 199.1 %reduce-scatter.26.cloned.1.call-start = ((), (), s32[]{:S(2)}) async-start(), calls=%async_computation.23 | async-start | bytes 1327104 | tf_op jit(solution)/shard_map/reduce_scatter | solution.py:362
  1245.6 250.2 %reduce-scatter.28.cloned.1.call-start = ((), (), s32[]{:S(2)}) async-start(), calls=%async_computation.24 | async-start | bytes 1327104 | tf_op jit(solution)/shard_map/reduce_scatter | solution.py:365
  1275.6 297.3 %reduce-scatter.30.cloned.1.call-start = ((), (), s32[]{:S(2)}) async-start(), calls=%async_computation.25 | async-start | bytes 3538944 | tf_op jit(solution)/shard_map/reduce_scatter | solution.py:368
  1300.6 349.8 %reduce-scatter.32.cloned.1.call-start = ((), (), s32[]{:S(2)}) async-start(), calls=%async_computation.26 | async-start | bytes 3538944 | tf_op jit(solution)/shard_map/reduce_scatter | solution.py:371
  1301.2 450.7 %reduce-scatter.20.cloned.1.call-start = ((), (), s32[]{:S(2)}) async-start(), calls=%async_computation.20 | async-start | bytes 15728640 | tf_op jit(solution)/shard_map/reduce_scatter | solution.py:333
  1317.9 434.0 %copy-start.20 = (bf16[512,1536]{1,0:T(8,128)(2,1)S(1)}, bf16[512,1536]{1,0:T(8,128)(2,1)}, u32[]{:S(2)}) copy-start(bf16[512,1536]{1,0:T(8,128)(2,1)} %param.19) | copy-start | bytes 4718596
  1317.9 434.0 %copy-start.127 = (f32[1536]{0:T(1024)S(1)}, f32[1536]{0:T(1024)}, u32[]{:S(2)}) copy-start(f32[1536]{0:T(1024)} %param.34) | copy-start | bytes 18436
  1317.9 434.0 %copy-start.158 = (f32[512]{0:T(512)S(1)}, f32[512]{0:T(512)}, u32[]{:S(2)}) copy-start(f32[512]{0:T(512)} %copy-done.157) | copy-start | bytes 6148
  1652.5 103.9 %copy-start.156 = (s32[512]{0:T(512)S(1)}, s32[512]{0:T(512)}, u32[]{:S(2)}) copy-start(s32[512]{0:T(512)} %copy-done.155) | copy-start | bytes 6148
  (185 other events, 1568.6 us)
Sparse Core Ops, SparseCore 0:
  24.4 49.0 all-gather.4
  322.7 99.6 reduce-scatter.13
  433.8 46.3 all-gather.6
  482.2 46.3 all-gather.8
  572.5 99.5 reduce-scatter.17
  674.5 58.8 reduce-scatter.15
  749.3 46.3 all-gather.10
  799.3 74.5 reduce-scatter.35
  877.5 73.4 reduce-scatter.33
  954.4 73.7 reduce-scatter.37
  1229.2 64.6 reduce-scatter.21
  1297.2 63.8 reduce-scatter.23
  1365.0 63.7 reduce-scatter.25
  1432.1 63.7 reduce-scatter.27
  1499.3 73.5 reduce-scatter.29
  1576.4 74.0 reduce-scatter.31
  1652.9 98.9 reduce-scatter.19
where the time goes:
time: 1830 us
  waiting for transfers between devices  757 us (41%)
  matrix products  645 us (35%)
  other arithmetic  303 us (17%)
  local copies, waits for them, and re-layouts  53.3 us (3%)
  blocking collectives  51.8 us (3%)
    reduce_scatter x1, waiting for transfers between devices, on_device(): lax.psum_scatter(jnp.dot(mixed_low, w_out, preferred_element_type=jnp.flo...  99.7 us
    reduce_scatter x1, waiting for transfers between devices, on_device(): lax.psum_scatter(lax.dot_general(d_joint_low, w_joint, contract_cols, pre...  99.4 us
    convert_element_type x4, other arithmetic, on_device(): d_scores = (probs_self * (d_probs - row_delta)).astype(jnp.bfloat16)  89.3 us
    reduce_scatter x1, waiting for transfers between devices, on_device(): lax.psum_scatter(lax.dot_general(d_gate_low, w_gate, contract_cols, prefe...  88.1 us
    reduce_scatter x1, waiting for transfers between devices, on_device(): lax.psum_scatter(grad_text_value.astype(jnp.bfloat16), 'dp', scatter_dime...  75.5 us
    reduce_scatter x1, waiting for transfers between devices, on_device(): lax.psum_scatter(grad_text_key.astype(jnp.bfloat16), 'dp', scatter_dimens...  75.5 us
    reduce_sum x8, other arithmetic, masked_softmax(): row_total = jnp.sum(exp_scores, -1, keepdims=True)  74.1 us
    dot_general x4, matrix products, on_device(): jnp.einsum('qhd,khd->hqk', d_self_block, value_low, preferred_element_typ...  71.4 us
  transfers between devices with their start and end apart: 17, of which 13 were waited for; matrix products, arithmetic and copies ran while one was open for 34% of the time, Pallas kernels for 0%

commit v1 on v0

v1 whole, which is shorter than its diff:
```python
import functools

import jax
import jax.numpy as jnp
from jax import lax
from jax.experimental import pallas as pl
from jax.experimental.pallas import tpu as pltpu
from jax.sharding import PartitionSpec as P

D = 1536
H = 24
HD = 64
TXT = 256
IMGS = 5
LANES = 128
BQ = 256
BK = 256
SEG = HD
LSE = HD + IMGS
OFF = 256.0
NT = (((1,), (1,)), ((), ()))


def modulated_norm(row_block, gain_vec, scale_vec):
    return (
        row_block
        * lax.rsqrt(jnp.mean(row_block * row_block, -1, keepdims=True) + 1e-05)
        * gain_vec
        * (1.0 + scale_vec)
    )


def lane_of(rows):
    return lax.broadcasted_iota(jnp.int32, (rows, LANES), 1)


def first_head(lane):
    return lane < HD


def swap_quarters(x, lane):
    low = (lane % 32) < 16
    return jnp.where(low, pltpu.roll(x, LANES - 16, 1), pltpu.roll(x, 16, 1))


def half_sums(x, lane):
    one = jnp.sum(jnp.where(first_head(lane), x, 0.0), -1, keepdims=True)
    two = jnp.sum(jnp.where(first_head(lane), 0.0, x), -1, keepdims=True)
    return jnp.where(first_head(lane), one, two)


def normed_heads(x, lane):
    return x * lax.rsqrt(half_sums(x * x, lane) * (1.0 / HD) + 1e-06)


def normed_heads_back(x, w, lane):
    r = lax.rsqrt(half_sums(x * x, lane) * (1.0 / HD) + 1e-06)
    return r * (w - x * (r * r) * (half_sums(w * x, lane) * (1.0 / HD)))


def turned(y, cos, sin, lane):
    return y * cos + swap_quarters(y, lane) * sin


def turned_back(dy, cos, sin, lane):
    return dy * cos + swap_quarters(dy * sin, lane)


def three_parts(x):
    one = x.astype(jnp.bfloat16).astype(jnp.float32)
    two = (x - one).astype(jnp.bfloat16).astype(jnp.float32)
    return one, two, x - one - two


def with_parts(base, x, lane, at):
    one, two, three = three_parts(x)
    return jnp.where(
        lane == at, one, jnp.where(lane == at + 1, two, jnp.where(lane == at + 2, three, base))
    )


def attend_kernel(
    bounds,
    gates,
    q_ref,
    k_ref,
    v_ref,
    tk_ref,
    tv_ref,
    cosq_ref,
    sinq_ref,
    cos_ref,
    sin_ref,
    qm_ref,
    km_ref,
    tm_ref,
    mixed_ref,
    os_ref,
    oc_ref,
    qs_ref,
    qc_ref,
    kh_ref,
    vh_ref,
    tkh_ref,
    tvh_ref,
):
    pair, block = pl.program_id(0), pl.program_id(1)
    bf16, f32 = jnp.bfloat16, jnp.float32

    @pl.when(block == 0)
    def _():
        lane = lane_of(BK)
        ones = jnp.where((lane >= HD) & (lane < HD + 3), 1.0, 0.0)

        def split(into, rows, x, rest):
            into[0, rows, :] = jnp.where(first_head(lane), x, rest).astype(bf16)
            into[1, rows, :] = jnp.where(first_head(lane), pltpu.roll(x, HD, 1), rest).astype(bf16)

        @pl.loop(0, k_ref.shape[0] // BK)
        def _(i):
            rows = pl.ds(pl.multiple_of(i * BK, BK), BK)
            key = turned(normed_heads(k_ref[rows, :], lane), cos_ref[rows, :], sin_ref[rows, :], lane)
            split(kh_ref, rows, key, km_ref[rows, :].astype(f32))
            split(vh_ref, rows, v_ref[rows, :], ones)

        @pl.loop(0, tk_ref.shape[0] // BK)
        def _(i):
            rows = pl.ds(pl.multiple_of(i * BK, BK), BK)
            split(tkh_ref, rows, normed_heads(tk_ref[rows, :], lane), tm_ref[rows, :].astype(f32))
            split(tvh_ref, rows, tv_ref[rows, :], ones)

    lane = lane_of(BQ)
    query = turned(normed_heads(q_ref[...], lane), cosq_ref[...], sinq_ref[...], lane) * (HD**-0.5)
    extra = qm_ref[...].astype(f32)
    heads = (
        jnp.where(first_head(lane), query, extra).astype(bf16),
        jnp.where(first_head(lane), pltpu.roll(query, HD, 1), extra).astype(bf16),
    )

    def run(keys, values, start, stop):
        def body(j, accs):
            rows = pl.ds(pl.multiple_of(j * BK, BK), BK)
            new = []
            for i in range(2):
                scores = lax.dot_general(heads[i], keys[i, rows, :], NT, preferred_element_type=f32)
                probs = jnp.exp(scores).astype(bf16)
                new.append(accs[i] + jnp.dot(probs, values[i, rows, :], preferred_element_type=f32))
            return tuple(new)

        zero = jnp.zeros((BQ, LANES), f32)
        accs = lax.fori_loop(start, stop, body, (zero, zero))
        outs, totals = [], []
        for i in range(2):
            total = accs[i][:, HD : HD + 1]
            outs.append(accs[i] / total)
            totals.append(jnp.log(total))
        return outs, totals

    self_out, self_total = run(kh_ref, vh_ref, bounds[0, block], bounds[1, block])
    cross_out, cross_total = run(tkh_ref, tvh_ref, bounds[2, block], bounds[3, block])
    for i in range(2):
        wide = heads[i].astype(f32)
        qs_ref[i] = with_parts(wide, -self_total[i], lane, LSE).astype(bf16)
        qc_ref[i] = with_parts(wide, -cross_total[i], lane, LSE).astype(bf16)
    both_self = jnp.where(first_head(lane), self_out[0], pltpu.roll(self_out[1], HD, 1))
    both_cross = jnp.where(first_head(lane), cross_out[0], pltpu.roll(cross_out[1], HD, 1))
    gate = jnp.where(first_head(lane), gates[2 * pair], gates[2 * pair + 1])
    os_ref[...] = both_self
    oc_ref[...] = both_cross
    mixed_ref[...] = (both_self + gate * both_cross).astype(bf16)


def attend_back_kernel(
    bounds,
    gates,
    dm_ref,
    os_ref,
    oc_ref,
    qs_ref,
    qc_ref,
    kh_ref,
    vh_ref,
    tkh_ref,
    tvh_ref,
    q_ref,
    k_ref,
    tk_ref,
    cosq_ref,
    sinq_ref,
    cos_ref,
    sin_ref,
    dq_ref,
    dk_ref,
    dv_ref,
    dtk_ref,
    dtv_ref,
    dh_ref,
    dk_acc,
    dv_acc,
    dtk_acc,
    dtv_acc,
    kt,
    tkt,
):
    pair, block = pl.program_id(0), pl.program_id(1)
    bf16, f32 = jnp.bfloat16, jnp.float32

    @pl.when(block == 0)
    def _():
        for acc in (dk_acc, dv_acc, dtk_acc, dtv_acc):
            acc[...] = jnp.zeros_like(acc)
        dh_ref[...] = jnp.zeros_like(dh_ref)
        for i in range(2):
            kt[i] = kh_ref[i].T
            tkt[i] = tkh_ref[i].T

    lane = lane_of(BQ)
    gate = jnp.where(first_head(lane), gates[2 * pair], gates[2 * pair + 1])
    d_mixed = dm_ref[...]
    both_cross = oc_ref[...]
    dh_ref[...] += jnp.sum((d_mixed * both_cross).reshape(1, BQ // 8, 8, LANES), 1)

    def cotangents(d_out, out):
        d_out = d_out.astype(bf16).astype(f32)
        terms = d_out * out
        one = jnp.sum(jnp.where(first_head(lane), terms, 0.0), -1, keepdims=True)
        two = jnp.sum(jnp.where(first_head(lane), 0.0, terms), -1, keepdims=True)
        zero = jnp.zeros_like(d_out)
        return (
            with_parts(jnp.where(first_head(lane), d_out, zero), -one, lane, HD).astype(bf16),
            with_parts(
                jnp.where(first_head(lane), pltpu.roll(d_out, HD, 1), zero), -two, lane, HD
            ).astype(bf16),
        )

    d_self = cotangents(d_mixed, os_ref[...])
    d_cross = cotangents(gate * d_mixed, both_cross)

    def run(queries, d_outs, keys, values, keys_t, dk, dv, start, stop, accs):
        def body(j, accs):
            rows = pl.ds(pl.multiple_of(j * BK, BK), BK)
            new = []
            for i in range(2):
                query = queries[i]
                scores = lax.dot_general(keys[i, rows, :], query, NT, preferred_element_type=f32)
                d_probs = lax.dot_general(
                    values[i, rows, :], d_outs[i], NT, preferred_element_type=f32
                )
                probs = jnp.exp(scores)
                d_scores = (probs * d_probs).astype(bf16)
                dv[i, rows, :] += jnp.dot(
                    probs.astype(bf16), d_outs[i], preferred_element_type=f32
                )
                dk[i, rows, :] += jnp.dot(d_scores, query, preferred_element_type=f32)
                new.append(
                    accs[i]
                    + jnp.dot(keys_t[i, :, rows], d_scores, preferred_element_type=f32)
                )
            return tuple(new)

        return lax.fori_loop(start, stop, body, accs)

    zero = jnp.zeros((LANES, BQ), f32)
    accs = run(
        qs_ref, d_self, kh_ref, vh_ref, kt, dk_acc, dv_acc, bounds[0, block], bounds[1, block], (zero, zero)
    )
    accs = run(
        qc_ref, d_cross, tkh_ref, tvh_ref, tkt, dtk_acc, dtv_acc, bounds[2, block], bounds[3, block], accs
    )
    d_query = jnp.where(first_head(lane), accs[0].T, pltpu.roll(accs[1].T, HD, 1)) * (HD**-0.5)
    d_query = turned_back(d_query, cosq_ref[...], sinq_ref[...], lane)
    dq_ref[...] = normed_heads_back(q_ref[...], d_query, lane).astype(bf16)

    @pl.when(block == pl.num_programs(1) - 1)
    def _():
        lane = lane_of(BK)

        def joined(acc, rows):
            return jnp.where(first_head(lane), acc[0, rows, :], pltpu.roll(acc[1, rows, :], HD, 1))

        @pl.loop(0, k_ref.shape[0] // BK)
        def _(i):
            rows = pl.ds(pl.multiple_of(i * BK, BK), BK)
            d_key = turned_back(joined(dk_acc, rows), cos_ref[rows, :], sin_ref[rows, :], lane)
            dk_ref[rows, :] = normed_heads_back(k_ref[rows, :], d_key, lane).astype(bf16)
            dv_ref[rows, :] = joined(dv_acc, rows).astype(bf16)

        @pl.loop(0, tk_ref.shape[0] // BK)
        def _(i):
            rows = pl.ds(pl.multiple_of(i * BK, BK), BK)
            dtk_ref[rows, :] = normed_heads_back(
                tk_ref[rows, :], joined(dtk_acc, rows), lane
            ).astype(bf16)
            dtv_ref[rows, :] = joined(dtv_acc, rows).astype(bf16)


def window(rows, at):
    return pl.BlockSpec((rows, LANES), at)


def attend(bounds, gates, joint, text, cos, sin, qm, km, tm):
    seq, slots = joint.shape[0], text.shape[0]
    pairs = joint.shape[1] // (3 * LANES)
    blocks = seq // BQ
    bf16, f32 = jnp.bfloat16, jnp.float32
    per_head = lambda rows: pl.BlockSpec((2, rows, LANES), lambda p, b, *_: (p, 0, 0))
    grid = pltpu.PrefetchScalarGridSpec(
        num_scalar_prefetch=2,
        grid=(pairs, blocks),
        in_specs=[
            window(BQ, lambda p, b, *_: (b, p)),
            window(seq, lambda p, b, *_: (0, pairs + p)),
            window(seq, lambda p, b, *_: (0, 2 * pairs + p)),
            window(slots, lambda p, b, *_: (0, p)),
            window(slots, lambda p, b, *_: (0, pairs + p)),
            window(BQ, lambda p, b, *_: (b, 0)),
            window(BQ, lambda p, b, *_: (b, 0)),
            window(seq, lambda p, b, *_: (0, 0)),
            window(seq, lambda p, b, *_: (0, 0)),
            window(BQ, lambda p, b, *_: (b, 0)),
            window(seq, lambda p, b, *_: (0, 0)),
            window(slots, lambda p, b, *_: (0, 0)),
        ],
        out_specs=[
            window(BQ, lambda p, b, *_: (b, p)),
            window(BQ, lambda p, b, *_: (b, p)),
            window(BQ, lambda p, b, *_: (b, p)),
            pl.BlockSpec((2, BQ, LANES), lambda p, b, *_: (p, b, 0)),
            pl.BlockSpec((2, BQ, LANES), lambda p, b, *_: (p, b, 0)),
            per_head(seq),
            per_head(seq),
            per_head(slots),
            per_head(slots),
        ],
    )
    wide = pairs * LANES
    held = lambda rows: jax.ShapeDtypeStruct((2 * pairs, rows, LANES), bf16)
    return pl.pallas_call(
        attend_kernel,
        grid_spec=grid,
        out_shape=[
            jax.ShapeDtypeStruct((seq, wide), bf16),
            jax.ShapeDtypeStruct((seq, wide), f32),
            jax.ShapeDtypeStruct((seq, wide), f32),
            held(seq),
            held(seq),
            held(seq),
            held(seq),
            held(slots),
            held(slots),
        ],
        compiler_params=pltpu.CompilerParams(dimension_semantics=("arbitrary", "arbitrary")),
        cost_estimate=pl.CostEstimate(
            flops=20_000_000_000, bytes_accessed=30_000_000, transcendentals=0
        ),
        name="attend",
    )(bounds, gates, joint, joint, joint, text, text, cos, sin, cos, sin, qm, km, tm)


def attend_back(bounds, gates, d_mixed, saved, joint, text, cos, sin):
    seq, slots = joint.shape[0], text.shape[0]
    pairs = joint.shape[1] // (3 * LANES)
    blocks = seq // BQ
    bf16, f32 = jnp.bfloat16, jnp.float32
    per_head = lambda rows: pl.BlockSpec((2, rows, LANES), lambda p, b, *_: (p, 0, 0))
    per_block = pl.BlockSpec((2, BQ, LANES), lambda p, b, *_: (p, b, 0))
    mine = window(BQ, lambda p, b, *_: (b, p))
    grid = pltpu.PrefetchScalarGridSpec(
        num_scalar_prefetch=2,
        grid=(pairs, blocks),
        in_specs=[
            mine,
            mine,
            mine,
            per_block,
            per_block,
            per_head(seq),
            per_head(seq),
            per_head(slots),
            per_head(slots),
            mine,
            window(seq, lambda p, b, *_: (0, pairs + p)),
            window(slots, lambda p, b, *_: (0, p)),
            window(BQ, lambda p, b, *_: (b, 0)),
            window(BQ, lambda p, b, *_: (b, 0)),
            window(seq, lambda p, b, *_: (0, 0)),
            window(seq, lambda p, b, *_: (0, 0)),
        ],
        out_specs=[
            mine,
            window(seq, lambda p, b, *_: (0, p)),
            window(seq, lambda p, b, *_: (0, p)),
            window(slots, lambda p, b, *_: (0, p)),
            window(slots, lambda p, b, *_: (0, p)),
            pl.BlockSpec((1, 8, LANES), lambda p, b, *_: (p, 0, 0)),
        ],
        scratch_shapes=[
            pltpu.VMEM((2, seq, LANES), f32),
            pltpu.VMEM((2, seq, LANES), f32),
            pltpu.VMEM((2, slots, LANES), f32),
            pltpu.VMEM((2, slots, LANES), f32),
            pltpu.VMEM((2, LANES, seq), bf16),
            pltpu.VMEM((2, LANES, slots), bf16),
        ],
    )
    wide = pairs * LANES
    return pl.pallas_call(
        attend_back_kernel,
        grid_spec=grid,
        out_shape=[
            jax.ShapeDtypeStruct((seq, wide), bf16),
            jax.ShapeDtypeStruct((seq, wide), bf16),
            jax.ShapeDtypeStruct((seq, wide), bf16),
            jax.ShapeDtypeStruct((slots, wide), bf16),
            jax.ShapeDtypeStruct((slots, wide), bf16),
            jax.ShapeDtypeStruct((pairs, 8, LANES), f32),
        ],
        compiler_params=pltpu.CompilerParams(dimension_semantics=("arbitrary", "arbitrary")),
        cost_estimate=pl.CostEstimate(
            flops=60_000_000_000, bytes_accessed=40_000_000, transcendentals=0
        ),
        name="attend_back",
    )(
        bounds, gates, d_mixed, *saved, joint, joint, text, cos, sin, cos, sin
    )


def swapped(value, axis, bit):
    size = lax.axis_size(axis)
    return lax.ppermute(value, axis, [(i, i ^ bit) for i in range(size)])


def gather_rows(mine):
    size = lax.axis_size("mp")
    if size != 4:
        return lax.all_gather(mine, "mp", axis=0, tiled=True)
    rows, me = mine.shape[0], lax.axis_index("mp")
    across = swapped(mine, "mp", 2)
    beside = swapped(mine, "mp", 1)
    diagonal = swapped(across, "mp", 1)
    out = jnp.zeros((4, rows, mine.shape[1]), mine.dtype)
    for part, bit in ((mine, 0), (beside, 1), (across, 2), (diagonal, 3)):
        out = lax.dynamic_update_slice(out, part[None], (me ^ bit, 0, 0))
    return out.reshape(4 * rows, mine.shape[1])


def scatter_rows(partial):
    size = lax.axis_size("mp")
    if size != 4:
        return lax.psum_scatter(partial, "mp", scatter_dimension=0, tiled=True).astype(jnp.float32)
    me = lax.axis_index("mp")
    quarters = partial.reshape(4, partial.shape[0] // 4, partial.shape[1])
    take = lambda bit: lax.dynamic_index_in_dim(quarters, me ^ bit, 0, keepdims=False)
    far = swapped(take(3), "mp", 1)
    near = swapped(take(1), "mp", 1)
    summed = (take(2).astype(jnp.float32) + far.astype(jnp.float32)).astype(jnp.bfloat16)
    other = swapped(summed, "mp", 2)
    return take(0).astype(jnp.float32) + near.astype(jnp.float32) + other.astype(jnp.float32)


def sum_over(value, axes):
    for axis in axes:
        bit = 1
        while bit < lax.axis_size(axis):
            value = value + swapped(value, axis, bit)
            bit *= 2
    return value


def on_device(
    hidden_in,
    text_states,
    modulation,
    image_lengths,
    text_lengths,
    positions,
    w_query,
    w_key,
    w_value,
    w_out,
    w_text_key,
    w_text_value,
    w_gate,
    w_up,
    w_down,
    attention_gain,
    feedforward_gain,
    head_gates,
    out_cotangent,
):
    highest = lax.Precision.HIGHEST
    bf16, f32 = jnp.bfloat16, jnp.float32
    contract_rows = (((0,), (0,)), ((), ()))
    contract_cols = (((1,), (1,)), ((), ()))
    local_rows = hidden_in.shape[0]
    shard_index = lax.axis_index("mp")
    seq_len = local_rows * lax.axis_size("mp")
    local_heads = w_query.shape[1] // HD
    local_width = local_heads * HD
    wide = -(-local_width // LANES) * LANES
    spare = wide - local_width
    slot_count = text_states.shape[0]
    image_ids = jnp.arange(IMGS, dtype=jnp.int32)
    token_ids = jnp.arange(seq_len, dtype=jnp.int32)
    image_ends = jnp.cumsum(image_lengths[0])
    image_starts = image_ends - image_lengths[0]
    image_of = jnp.sum((token_ids[:, None] >= image_ends[None, :]).astype(jnp.int32), 1)
    select_all = (image_of[:, None] == image_ids[None, :]).astype(f32)
    select_mine = lax.dynamic_slice_in_dim(select_all, shard_index * local_rows, local_rows, 0)
    per_token = jnp.dot(select_mine, modulation[0], precision=highest)
    scale_attn = per_token[:, 0:D]
    gate_attn = per_token[:, D : 2 * D]
    scale_ffn = per_token[:, 2 * D : 3 * D]
    gate_ffn = per_token[:, 3 * D :]

    def lanes(columns):
        rows = columns.shape[0]
        return jnp.pad(columns, ((0, 0), (HD, LANES - HD - columns.shape[1]))).astype(bf16)

    slot_ids = jnp.arange(slot_count, dtype=jnp.int32)
    slot_live = (slot_ids % TXT)[:, None] < text_lengths[0][None, :]
    slot_fits = ((slot_ids // TXT)[:, None] == image_ids[None, :]) & slot_live
    three = lambda rows: jnp.ones((rows, 3), f32)
    query_lanes = lanes(select_all)
    key_lanes = lanes(jnp.concatenate([(select_all - 1.0) * OFF, three(seq_len)], 1))
    text_lanes = lanes(
        jnp.concatenate([jnp.where(slot_fits, 0.0, -OFF), three(slot_count)], 1)
    )
    block_first = jnp.arange(seq_len // BQ, dtype=jnp.int32) * BQ
    in_first = jnp.sum((block_first[:, None] >= image_ends[None, :]).astype(jnp.int32), 1)
    in_last = jnp.sum(((block_first + BQ - 1)[:, None] >= image_ends[None, :]).astype(jnp.int32), 1)
    pick = lambda values, at: jnp.sum(
        jnp.where(at[:, None] == image_ids[None, :], values[None, :], 0), 1
    )
    bounds = jnp.stack(
        [
            pick(image_starts, in_first) // BK,
            (pick(image_ends, in_last) + BK - 1) // BK,
            in_first,
            in_last + 1,
        ]
    ).astype(jnp.int32)

    quarter = HD // 4
    frequency = 10000.0 ** (-jnp.arange(quarter, dtype=f32) / quarter)
    angle_row = positions[0].astype(f32)[:, None] * frequency[None, :]
    angle_col = positions[1].astype(f32)[:, None] * frequency[None, :]
    cos_row, sin_row, cos_col, sin_col = (
        jnp.cos(angle_row),
        jnp.sin(angle_row),
        jnp.cos(angle_col),
        jnp.sin(angle_col),
    )
    cos = jnp.concatenate([cos_row, cos_row, cos_col, cos_col] * 2, 1)
    sin = jnp.concatenate([-sin_row, sin_row, -sin_col, sin_col] * 2, 1)

    hidden_float = hidden_in.astype(f32)
    normed_one, back_norm_one = jax.vjp(modulated_norm, hidden_float, attention_gain, scale_attn)
    rows_attn = gather_rows(normed_one.astype(bf16))
    tanh_ffn = jnp.tanh(gate_ffn)
    cotangent = out_cotangent.astype(f32)
    d_ffn_all = gather_rows((cotangent * tanh_ffn).astype(bf16))

    widen = lambda w: jnp.pad(w, ((0, 0), (0, spare))) if spare else w
    w_joint = jnp.concatenate([widen(w_query), widen(w_key), widen(w_value)], 1)
    w_text = jnp.concatenate([widen(w_text_key), widen(w_text_value)], 1)
    w_out_wide = jnp.pad(w_out, ((0, spare), (0, 0))) if spare else w_out
    text_joint = jnp.dot(text_states, w_text, preferred_element_type=f32)
    joint = jnp.dot(rows_attn, w_joint, preferred_element_type=f32)
    gate_mine = lax.dynamic_slice_in_dim(head_gates, shard_index * local_heads, local_heads, 0)
    gate_tanh = jnp.tanh(gate_mine)
    gates = jnp.pad(gate_tanh, (0, wide // HD - local_heads))
    mixed_low, *saved = attend(
        bounds, gates, joint, text_joint, cos, sin, query_lanes, key_lanes, text_lanes
    )

    attention_out = scatter_rows(jnp.dot(mixed_low, w_out_wide, preferred_element_type=f32).astype(bf16))
    tanh_attn = jnp.tanh(gate_attn)
    after_attn = hidden_float + tanh_attn * attention_out
    normed_two, back_norm_two = jax.vjp(modulated_norm, after_attn, feedforward_gain, scale_ffn)
    rows_ffn = gather_rows(normed_two.astype(bf16))
    gate_pre = jnp.dot(rows_ffn, w_gate, preferred_element_type=f32)
    up_pre = jnp.dot(rows_ffn, w_up, preferred_element_type=f32)
    sigmoid_gate = jax.nn.sigmoid(gate_pre)
    activated = gate_pre * sigmoid_gate
    inner_low = (activated * up_pre).astype(bf16)
    d_inner = lax.dot_general(d_ffn_all, w_down, contract_cols, preferred_element_type=f32)
    d_gate_low = (d_inner * up_pre * sigmoid_gate * (1.0 + gate_pre * (1.0 - sigmoid_gate))).astype(
        bf16
    )
    d_up_low = (d_inner * activated).astype(bf16)
    d_normed_two = scatter_rows(
        (
            lax.dot_general(d_gate_low, w_gate, contract_cols, preferred_element_type=f32)
            + lax.dot_general(d_up_low, w_up, contract_cols, preferred_element_type=f32)
        ).astype(bf16)
    )
    ffn_out = scatter_rows(jnp.dot(inner_low, w_down, preferred_element_type=f32).astype(bf16))
    block_out = (after_attn + tanh_ffn * ffn_out).astype(bf16)
    d_gate_ffn = cotangent * ffn_out * (1.0 - tanh_ffn * tanh_ffn)
    grad_down_t = lax.dot_general(d_ffn_all, inner_low, contract_rows, preferred_element_type=f32)
    grad_gate = lax.dot_general(rows_ffn, d_gate_low, contract_rows, preferred_element_type=f32)
    grad_up = lax.dot_general(rows_ffn, d_up_low, contract_rows, preferred_element_type=f32)

    def sum_packs(*grads):
        joined = jnp.concatenate([g.astype(bf16) for g in grads], 1)
        summed = lax.psum_scatter(joined, "dp", scatter_dimension=0, tiled=True).astype(f32)
        parts, at = [], 0
        for g in grads:
            parts.append(summed[:, at : at + g.shape[1]])
            at += g.shape[1]
        return parts

    out_gate, out_up, out_down_t = sum_packs(grad_gate, grad_up, grad_down_t)

    d_after_norm, grad_ffn_gain, d_scale_ffn = back_norm_two(d_normed_two)
    d_after = cotangent + d_after_norm
    d_attn_low = (d_after * tanh_attn).astype(bf16)
    d_gate_attn = d_after * attention_out * (1.0 - tanh_attn * tanh_attn)
    d_attn_all = gather_rows(d_attn_low)
    grad_out_t = lax.dot_general(d_attn_all, mixed_low, contract_rows, preferred_element_type=f32)
    d_mixed = lax.dot_general(d_attn_all, w_out_wide, contract_cols, preferred_element_type=f32)
    d_query, d_key, d_value, d_text_key, d_text_value, d_heads = attend_back(
        bounds, gates, d_mixed, saved, joint, text_joint, cos, sin
    )
    grad_heads = jnp.sum(d_heads, 1).reshape(wide // HD, HD).sum(1)[:local_heads]
    grad_heads = grad_heads * (1.0 - gate_tanh * gate_tanh)
    narrow = lambda d: d[:, :local_width]
    d_text_low = jnp.concatenate([narrow(d_text_key), narrow(d_text_value)], 1)
    grad_text = lax.dot_general(text_states, d_text_low, contract_rows, preferred_element_type=f32)
    (out_text,) = sum_packs(grad_text)
    d_joint_low = jnp.concatenate([d_query, d_key, d_value], 1)
    d_normed_one = scatter_rows(
        lax.dot_general(d_joint_low, w_joint, contract_cols, preferred_element_type=f32).astype(bf16)
    )
    d_joint_low = jnp.concatenate([narrow(d_query), narrow(d_key), narrow(d_value)], 1)
    grad_joint = lax.dot_general(rows_attn, d_joint_low, contract_rows, preferred_element_type=f32)
    out_joint, out_out_t = sum_packs(grad_joint, narrow(grad_out_t))

    d_hidden_norm, grad_attn_gain, d_scale_attn = back_norm_one(d_normed_one)
    input_grad = (d_after + d_hidden_norm).astype(bf16)
    d_per_token = jnp.concatenate([d_scale_attn, d_gate_attn, d_scale_ffn, d_gate_ffn], 1)
    mod_partial = lax.dot_general(select_mine, d_per_token, contract_rows, precision=highest)
    modulation_grad = sum_over(mod_partial, ("mp",))[None]
    heads_full = lax.dynamic_update_slice(
        jnp.zeros((H,), f32), grad_heads, (shard_index * local_heads,)
    )
    small = jnp.concatenate([grad_attn_gain, grad_ffn_gain, heads_full])
    small = sum_over(small, ("mp", "dp"))
    return (
        block_out,
        input_grad,
        modulation_grad,
        out_joint[:, 0:local_width],
        out_joint[:, local_width : 2 * local_width],
        out_joint[:, 2 * local_width :],
        out_out_t.T,
        out_text[:, 0:local_width],
        out_text[:, local_width:],
        out_gate,
        out_up,
        out_down_t.T,
        small[0:D],
        small[D : 2 * D],
        small[2 * D :],
    )


def solution(mesh):
    placed = (
        P(("dp", "mp"), None),
        P("dp", None),
        P("dp", None, None),
        P("dp", None),
        P("dp", None),
        P(None, "dp"),
        P(None, "mp"),
        P(None, "mp"),
        P(None, "mp"),
        P("mp", None),
        P(None, "mp"),
        P(None, "mp"),
        P(None, "mp"),
        P(None, "mp"),
        P("mp", None),
        P(),
        P(),
        P(),
        P(("dp", "mp"), None),
    )
    return jax.shard_map(
        on_device,
        mesh=mesh,
        in_specs=placed,
        out_specs=(
            P(("dp", "mp"), None),
            P(("dp", "mp"), None),
            P("dp", None, None),
            P("dp", "mp"),
            P("dp", "mp"),
            P("dp", "mp"),
            P("mp", "dp"),
            P("dp", "mp"),
            P("dp", "mp"),
            P("dp", "mp"),
            P("dp", "mp"),
            P("mp", "dp"),
            P(),
            P(),
            P(),
        ),
        check_vma=False,
    )
```

time: 1830 us -> 1110 us (0.61)
  matrix products: 645 us -> 189 us
  waiting for transfers between devices: 757 us -> 453 us
  Pallas kernels: 0 us -> 253 us
  other arithmetic: 303 us -> 59 us
  local copies, waits for them, and re-layouts: 53.3 us -> 115 us
  blocking collectives: 51.8 us -> 0 us
    reduce_scatter x13 -> x1, waiting for transfers between devices: 661 us -> 108 us  [sum_packs(): lax.psum_scatter(joined, 'dp', scatter_dimension=0, tiled=True).astype(f32)]
    dot_general x56 -> x8, matrix products: 526 us -> 75.7 us  [the longest x1 14.1 us: on_device(): text_joint = jnp.dot(text_states, w_text, preferred_element_type=f32)]
    pallas_call x0 -> x2, Pallas kernels: none -> 253 us  [the longest x1 134 us: attend_back(): pl.pallas_call(attend_back_kernel, grid_spec=grid, out_shape=[jax.ShapeDt...]
    ppermute x0 -> x31, waiting for transfers between devices: none -> 241 us  [swapped(): return lax.ppermute(value, axis, [(i, i ^ bit) for i in range(size)])]
    convert_element_type x22 -> x8, other arithmetic: 167 us -> 6.81 us  [the longest x4 2.76 us: scatter_rows(): (take(2).astype(jnp.float32) + far.astype(jnp.float32)).astype(jnp.bfloat16)]
    unnamed x17 -> x5, waiting for transfers between devices: 1.8 us -> 104 us
    all_gather x4 -> x0, waiting for transfers between devices: 94.3 us -> none  [the longest x1 45.9 us: on_device(): lax.all_gather(normed_two.astype(jnp.bfloat16), 'mp', axis=0, tiled=True)]
    reduce_sum x15 -> x5, other arithmetic: 78.6 us -> 0.72 us  [the longest x2 0.4 us: on_device(): jnp.sum(jnp.where(at[:, None] == image_ids[None, :], values[None, :], 0), 1)]
  transfers between devices with their start and end apart: 17 -> 34, of which waited for: 13 -> 18; matrix products, arithmetic and copies ran while one was open for 34% -> 18% of each run, Pallas kernels for 0% -> 0%
where the time goes in v1:
time: 1110 us; the launch traced here: 1100 us
  waiting for transfers between devices  453 us (41%)
  Pallas kernels  253 us (23%)
  matrix products  189 us (17%)
  local copies, waits for them, and re-layouts  115 us (10%)
  other arithmetic  59 us (5%)
  starting transfers between devices  18.7 us (2%)
  between operations  15.2 us (1%)
    ppermute x31, waiting for transfers between devices, swapped(): return lax.ppermute(value, axis, [(i, i ^ bit) for i in range(size)])  241 us
    pallas_call x1, Pallas kernels, attend_back(): pl.pallas_call(attend_back_kernel, grid_spec=grid, out_shape=[jax.ShapeDt...  134 us
    pallas_call x1, Pallas kernels, attend(): pl.pallas_call(attend_kernel, grid_spec=grid, out_shape=[jax.ShapeDtypeSt...  119 us
    reduce_scatter x1, waiting for transfers between devices, sum_packs(): lax.psum_scatter(joined, 'dp', scatter_dimension=0, tiled=True).astype(f32)  108 us
    unnamed x5, waiting for transfers between devices  104 us
    unnamed x148, local copies, waits for them, and re-layouts  64.7 us
  transfers between devices with their start and end apart: 34, of which 18 were waited for; matrix products, arithmetic and copies ran while one was open for 18% of the time, Pallas kernels for 0%

profile of v1, /device:TPU:0, one launch (start us, length us, event | category | flops | bytes accessed | tf_op | source)
XLA Modules:
  0.0 1102.8 jit_solution(10386358787428449881)
XLA Ops:
  32.9 10.1 multiply_sine_fusion
  43.0 8.0 concatenate.39.cosq_ref.cos_ref
  51.8 14.1 %fusion.14.tk_ref.tv_ref = f32[1280,768]{1,0:T(8,128)} fusion(bf16[1280,4096]{1,0:T(8,128)(2,1)} %param.20, bf16[4096,384]{1,0:T(8,128)(2,1)} %param.30, bf16[4096,384]{1,0:T(8,128)(2,1)} %param.29), kind=kOutput, calls=%fused_computation.39 | convolution fusion | flops 8065646592 | bytes 20709376 | tf_op jit(solution)/shard_map/dot_general | solution.py:568
  65.9 7.7 concatenate.40.sinq_ref.sin_ref
  87.3 12.6 %fusion.79.q_ref.k_ref.v_ref = f32[2048,1152]{1,0:T(8,128)} fusion(bf16[2048,1536]{1,0:T(8,128)(2,1)} %bitcast.183, bf16[1536,1152]{1,0:T(8,128)(2,1)S(1)} %constant_dynamic-update-slice_fusion), kind=kOutput, calls=%fused_computation.202 | convolution fusion | flops 7247757312 | bytes 19267584 | tf_op jit(solution)/shard_map/dot_general | solution.py:569
  99.9 118.7 %attend.1 = (bf16[2048,384]{1,0:T(8,128)(2,1)}, f32[2048,384]{1,0:T(8,128)}, f32[2048,384]{1,0:T(8,128)}, bf16[6,2048,128]{2,1,0:T(8,128)(2,1)}, bf16[6,2048,128...) custom-call(s32[4,8]{1,0:T(4,128)} %pad_add_fusion.bounds, ...), custom_call_target="tpu_custom_call" | custom-call | flops 20000000000 | bytes 30000000 | tf_op jit(solution)/shard_map/attend/pallas_call | solution.py:338
  235.9 29.6 %collective-permute-done.5 = bf16[512,1536]{1,0:T(8,128)(2,1)S(1)} collective-permute-done((bf16[512,1536]{1,0:T(8,128)(2,1)S(1)}, bf16[512,1536]{1,0:T(8,128)(2,1)S(1)}, u32[]{:S(2)}, u32[]{:S(2)}) %collective-permute-start.5) | collective-permute-done | bytes 1572896 | tf_op jit(solution)/shard_map/ppermute | solution.py:430
  272.5 26.8 %collective-permute-done.13 = bf16[512,1536]{1,0:T(8,128)(2,1)} collective-permute-done((bf16[512,1536]{1,0:T(8,128)(2,1)}, bf16[512,1536]{1,0:T(8,128)(2,1)}, u32[]{:S(2)}, u32[]{:S(2)}) %collective-permute-start.13) | collective-permute-done | bytes 1572896 | tf_op jit(solution)/shard_map/ppermute | solution.py:430
  303.1 29.1 %collective-permute-done.7 = bf16[512,1536]{1,0:T(8,128)(2,1)S(1)} collective-permute-done((bf16[512,1536]{1,0:T(8,128)(2,1)S(1)}, bf16[512,1536]{1,0:T(8,128)(2,1)S(1)}, u32[]{:S(2)}, u32[]{:S(2)}) %collective-permute-start.7) | collective-permute-done | bytes 1572896 | tf_op jit(solution)/shard_map/ppermute | solution.py:430
  336.5 8.8 fusion.81
  345.3 9.0 fusion.80
  354.4 18.7 %multiply_convert_fusion = (bf16[2048,1024]{1,0:T(8,128)(2,1)}, bf16[2048,1024]{1,0:T(8,128)(2,1)}, bf16[2048,1024]{1,0:T(8,128)(2,1)}) fusion(f32[2048,1024]{1,0:T(8,128)} %fusion.80, f32[2048,1024]{1,0:T(8,128)} %fusion.81, bf16[2048,1536]{1,0:T(8,128)(2,1)} %bitcast.187, bf16[1024,1536]{1,0:T(8,128)(2,1)S(1)} %copy-done), kind=kOutput, calls=%fused_computation.10 | convolution fusion | flops 6473908224 | bytes 38797312 | tf_op jit(solution)/shard_map/dot_general | solution.py:587
  373.0 12.4 %fusion.82 = f32[2048,1536]{1,0:T(8,128)} fusion(bf16[2048,1024]{1,0:T(8,128)(2,1)} %get-tuple-element.130, bf16[1536,1024]{1,0:T(8,128)(2,1)} %param.31), kind=kOutput, calls=%fused_computation.205 | convolution fusion | flops 6442450944 | bytes 19922944 | tf_op jit(solution)/shard_map/dot_general | solution.py:594
  385.5 11.3 %add_convert_fusion = bf16[2048,1536]{1,0:T(8,128)(2,1)S(1)} fusion(f32[2048,1536]{1,0:T(8,128)} %fusion.82, bf16[2048,1024]{1,0:T(8,128)(2,1)} %get-tuple-element.129, bf16[1536,1024]{1,0:T(8,128)(2,1)S(1)} %copy-done.47), kind=kOutput, calls=%fused_computation.8 | convolution fusion | flops 6448742400 | bytes 26214400 | tf_op jit(solution)/shard_map/dot_general | solution.py:595
  401.2 9.4 convolution_convert_fusion.2
  419.2 34.7 %collective-permute-done.17 = bf16[512,1536]{1,0:T(8,128)(2,1)S(1)} collective-permute-done((bf16[512,1536]{1,0:T(8,128)(2,1)S(1)}, bf16[512,1536]{1,0:T(8,128)(2,1)S(1)}, u32[]{:S(2)}, u32[]{:S(2)}) %collective-permute-start.17) | collective-permute-done | bytes 1572896 | tf_op jit(solution)/shard_map/ppermute | solution.py:430
  458.9 27.8 %collective-permute-done.11 = bf16[512,1536]{1,0:T(8,128)(2,1)S(1)} collective-permute-done((bf16[512,1536]{1,0:T(8,128)(2,1)S(1)}, bf16[512,1536]{1,0:T(8,128)(2,1)S(1)}, u32[]{:S(2)}, u32[]{:S(2)}) %collective-permute-start.11) | collective-permute-done | bytes 1572896 | tf_op jit(solution)/shard_map/ppermute | solution.py:430
  487.9 8.9 fusion.24
  499.4 35.2 %collective-permute-done.19 = bf16[512,1536]{1,0:T(8,128)(2,1)S(1)} collective-permute-done((bf16[512,1536]{1,0:T(8,128)(2,1)S(1)}, bf16[512,1536]{1,0:T(8,128)(2,1)S(1)}, u32[]{:S(2)}, u32[]{:S(2)}) %collective-permute-start.19) | collective-permute-done | bytes 1572896 | tf_op jit(solution)/shard_map/ppermute | solution.py:430
  547.0 134.2 %attend_back.1 = (bf16[2048,384]{1,0:T(8,128)(2,1)}, bf16[2048,384]{1,0:T(8,128)(2,1)}, bf16[2048,384]{1,0:T(8,128)(2,1)}, bf16[1280,384]{1,0:T(8,128)(2,1)}, bf...) custom-call(s32[4,8]{1,0:T(4,128)} %pad_add_fusion.bounds, f32[6]{0:T(128)} %dynamic-slice_tanh_fusion.gates, ...), custom_call_target="tpu_custom_call" | custom-call | flops 60000002048 | bytes 40000000 | tf_op jit(solution)/shard_map/attend_back/pallas_call | solution.py:407
  686.0 10.1 convolution_convert_fusion
  698.6 6.6 copy.82
  705.3 10.4 convolution_convert_fusion.5
  715.8 9.3 convolution_convert_fusion.6
  725.1 7.3 convolution_convert_fusion.7
  736.7 12.7 %copy.84 = bf16[1536,3072]{1,0:T(8,128)(2,1)} copy(bf16[1536,3072]{0,1:T(8,128)(2,1)} %pad_maximum_fusion) | data formatting | bytes 18874368
  750.8 15.0 %fusion.13 = bf16[4096,768]{0,1:T(8,128)(2,1)} fusion(bf16[1280,4096]{1,0:T(8,128)(2,1)} %param.20, bf16[1280,384]{1,0:T(8,128)(2,1)S(1)} %copy-done.52, bf16[1280,384]{1,0:T(8,128)(2,1)S(1)} %copy-done.51), kind=kOutput, calls=%fused_computation.29 | convolution fusion | flops 8060141568 | bytes 18743296 | tf_op jit(solution)/shard_map/dot_general | solution.py:630
  765.8 11.5 %convolution_convert_fusion.1 = bf16[2048,1536]{1,0:T(8,128)(2,1)S(1)} fusion(bf16[2048,1152]{1,0:T(8,128)(2,1)} %copy-done.29, bf16[1536,1152]{1,0:T(8,128)(2,1)} %copy-done.31), kind=kOutput, calls=%fused_computation.16 | convolution fusion | flops 7250903040 | bytes 14548992 | tf_op jit(solution)/shard_map/dot_general | solution.py:634
  784.6 36.0 %collective-permute-done.23 = bf16[512,1536]{1,0:T(8,128)(2,1)} collective-permute-done((bf16[512,1536]{1,0:T(8,128)(2,1)}, bf16[512,1536]{1,0:T(8,128)(2,1)}, u32[]{:S(2)}, u32[]{:S(2)}) %collective-permute-start.23) | collective-permute-done | bytes 1572896 | tf_op jit(solution)/shard_map/ppermute | solution.py:430
  832.1 8.6 fusion
  863.8 103.8 %reduce-scatter.12.cloned.1.call-done = bf16[192,3072]{1,0:T(8,128)(2,1)} async-done(((bf16[1536,3072]{1,0:T(8,128)(2,1)}), bf16[192,3072]{1,0:T(8,128)(2,1)}) %reduce-scatter.12.cloned.1.call-update) | async-done | bytes 1179664
  980.8 107.9 %reduce-scatter.8.cloned.1.call-done = bf16[512,768]{0,1:T(8,128)(2,1)} async-done(((bf16[4096,768]{0,1:T(8,128)(2,1)}), bf16[512,768]{0,1:T(8,128)(2,1)}) %reduce-scatter.8.cloned.1.call-update) | async-done | bytes 786448 | tf_op jit(solution)/shard_map/reduce_scatter | solution.py:607
  (300 shorter events, 181.4 us)
Async XLA Ops:
  7.2 851.5 %reduce-scatter.10.cloned.1.call-start = ((), (), s32[]{:S(2)}) async-start(), calls=%async_computation.4 | async-start | bytes 5308416
  27.1 52.3 %collective-permute-start = (bf16[512,1536]{1,0:T(8,128)(2,1)}, bf16[512,1536]{1,0:T(8,128)(2,1)}, u32[]{:S(2)}, u32[]{:S(2)}) collective-permute-start(bf16[512,1536]{1,0:T(8,128)(2,1)} %get-tuple-element.124), channel_id=1, source_target_pairs={{0,1},{1,0},{2,3},{3,2},{4,5},{5,4},{6,7},{7,6},{8,9},{9,8},{10,11... | collective-permute-start | bytes 4718600 | tf_op jit(solution)/shard_map/ppermute | solution.py:430
  27.6 50.2 %collective-permute-start.1 = (bf16[512,1536]{1,0:T(8,128)(2,1)}, bf16[512,1536]{1,0:T(8,128)(2,1)}, u32[]{:S(2)}, u32[]{:S(2)}) collective-permute-start(bf16[512,1536]{1,0:T(8,128)(2,1)} %get-tuple-element.124), channel_id=1, source_target_pairs={{0,2},{1,3},{2,0},{3,1},{4,6},{5,7},{6,4},{7,5},{8,10},{9,11},{10,... | collective-permute-start | bytes 4718600 | tf_op jit(solution)/shard_map/ppermute | solution.py:430
  77.9 8.1 collective-permute-start.2
  224.2 3.5 collective-permute-start.4
  224.6 11.3 %collective-permute-start.3 = (bf16[512,1536]{1,0:T(8,128)(2,1)S(1)}, bf16[512,1536]{1,0:T(8,128)(2,1)S(1)}, u32[]{:S(2)}, u32[]{:S(2)}) collective-permute-start(bf16[512,1536]{1,0:T(8,128)(2,1)S(1)} %get-tuple-element.140), channel_id=1, source_target_pairs={{0,1},{1,0},{2,3},{3,2},{4,5},{5,4},{6,7},{7,6},{8,9},{9,8},{10,11... | collective-permute-start | bytes 4718600 | tf_op jit(solution)/shard_map/ppermute | solution.py:430
  228.1 37.3 %collective-permute-start.5 = (bf16[512,1536]{1,0:T(8,128)(2,1)S(1)}, bf16[512,1536]{1,0:T(8,128)(2,1)S(1)}, u32[]{:S(2)}, u32[]{:S(2)}) collective-permute-start(bf16[512,1536]{1,0:T(8,128)(2,1)S(1)} %fusion.35), channel_id=1, source_target_pairs={{0,2},{1,3},{2,0},{3,1},{4,6},{5,7},{6,4},{7,5},{8,10},{9,11},{10,... | collective-permute-start | bytes 4718600 | tf_op jit(solution)/shard_map/ppermute | solution.py:430
  234.2 65.1 %collective-permute-start.13 = (bf16[512,1536]{1,0:T(8,128)(2,1)}, bf16[512,1536]{1,0:T(8,128)(2,1)}, u32[]{:S(2)}, u32[]{:S(2)}) collective-permute-start(bf16[512,1536]{1,0:T(8,128)(2,1)} %get-tuple-element.118), channel_id=1, source_target_pairs={{0,2},{1,3},{2,0},{3,1},{4,6},{5,7},{6,4},{7,5},{8,10},{9,11},{10,... | collective-permute-start | bytes 4718600 | tf_op jit(solution)/shard_map/ppermute | solution.py:430
  235.9 63.9 %collective-permute-start.12 = (bf16[512,1536]{1,0:T(8,128)(2,1)}, bf16[512,1536]{1,0:T(8,128)(2,1)}, u32[]{:S(2)}, u32[]{:S(2)}) collective-permute-start(bf16[512,1536]{1,0:T(8,128)(2,1)} %get-tuple-element.118), channel_id=1, source_target_pairs={{0,1},{1,0},{2,3},{3,2},{4,5},{5,4},{6,7},{7,6},{8,9},{9,8},{10,11... | collective-permute-start | bytes 4718600 | tf_op jit(solution)/shard_map/ppermute | solution.py:430
  272.2 60.0 %collective-permute-start.7 = (bf16[512,1536]{1,0:T(8,128)(2,1)S(1)}, bf16[512,1536]{1,0:T(8,128)(2,1)S(1)}, u32[]{:S(2)}, u32[]{:S(2)}) collective-permute-start(bf16[512,1536]{1,0:T(8,128)(2,1)S(1)} %get-tuple-element.120), channel_id=1, source_target_pairs={{0,2},{1,3},{2,0},{3,1},{4,6},{5,7},{6,4},{7,5},{8,10},{9,11},{10,... | collective-permute-start | bytes 4718600 | tf_op jit(solution)/shard_map/ppermute | solution.py:430
  299.2 32.9 %collective-permute-start.14 = (bf16[512,1536]{1,0:T(8,128)(2,1)}, bf16[512,1536]{1,0:T(8,128)(2,1)S(1)}, u32[]{:S(2)}, u32[]{:S(2)}) collective-permute-start(bf16[512,1536]{1,0:T(8,128)(2,1)} %collective-permute-done.13), channel_id=1, source_target_pairs={{0,1},{1,0},{2,3},{3,2},{4,5},{5,4},{6,7},{7,6},{8,9},{9,8},{10,11... | collective-permute-start | bytes 4718600 | tf_op jit(solution)/shard_map/ppermute | solution.py:430
  299.2 33.1 %collective-permute-start.6 = (bf16[512,1536]{1,0:T(8,128)(2,1)S(1)}, bf16[512,1536]{1,0:T(8,128)(2,1)S(1)}, u32[]{:S(2)}, u32[]{:S(2)}) collective-permute-start(bf16[512,1536]{1,0:T(8,128)(2,1)S(1)} %get-tuple-element.120), channel_id=1, source_target_pairs={{0,1},{1,0},{2,3},{3,2},{4,5},{5,4},{6,7},{7,6},{8,9},{9,8},{10,11... | collective-permute-start | bytes 4718600 | tf_op jit(solution)/shard_map/ppermute | solution.py:430
  332.2 3.4 collective-permute-start.8
  400.7 11.8 %collective-permute-start.16 = (bf16[512,1536]{1,0:T(8,128)(2,1)S(1)}, bf16[512,1536]{1,0:T(8,128)(2,1)S(1)}, u32[]{:S(2)}, u32[]{:S(2)}) collective-permute-start(bf16[512,1536]{1,0:T(8,128)(2,1)S(1)} %get-tuple-element.137), channel_id=1, source_target_pairs={{0,1},{1,0},{2,3},{3,2},{4,5},{5,4},{6,7},{7,6},{8,9},{9,8},{10,11... | collective-permute-start | bytes 4718600 | tf_op jit(solution)/shard_map/ppermute | solution.py:430
  412.0 5.0 collective-permute-start.10
  412.0 7.2 collective-permute-start.15
  416.7 37.3 %collective-permute-start.17 = (bf16[512,1536]{1,0:T(8,128)(2,1)S(1)}, bf16[512,1536]{1,0:T(8,128)(2,1)S(1)}, u32[]{:S(2)}, u32[]{:S(2)}) collective-permute-start(bf16[512,1536]{1,0:T(8,128)(2,1)S(1)} %fusion.31), channel_id=1, source_target_pairs={{0,2},{1,3},{2,0},{3,1},{4,6},{5,7},{6,4},{7,5},{8,10},{9,11},{10,... | collective-permute-start | bytes 4718600 | tf_op jit(solution)/shard_map/ppermute | solution.py:430
  417.0 41.9 %collective-permute-start.9 = (bf16[512,1536]{1,0:T(8,128)(2,1)}, bf16[512,1536]{1,0:T(8,128)(2,1)S(1)}, u32[]{:S(2)}, u32[]{:S(2)}) collective-permute-start(bf16[512,1536]{1,0:T(8,128)(2,1)} %get-tuple-element.138), channel_id=1, source_target_pairs={{0,1},{1,0},{2,3},{3,2},{4,5},{5,4},{6,7},{7,6},{8,9},{9,8},{10,11... | collective-permute-start | bytes 4718600 | tf_op jit(solution)/shard_map/ppermute | solution.py:430
  417.4 69.3 %collective-permute-start.11 = (bf16[512,1536]{1,0:T(8,128)(2,1)S(1)}, bf16[512,1536]{1,0:T(8,128)(2,1)S(1)}, u32[]{:S(2)}, u32[]{:S(2)}) collective-permute-start(bf16[512,1536]{1,0:T(8,128)(2,1)S(1)} %fusion.33), channel_id=1, source_target_pairs={{0,2},{1,3},{2,0},{3,1},{4,6},{5,7},{6,4},{7,5},{8,10},{9,11},{10,... | collective-permute-start | bytes 4718600 | tf_op jit(solution)/shard_map/ppermute | solution.py:430
  499.1 35.5 %collective-permute-start.19 = (bf16[512,1536]{1,0:T(8,128)(2,1)S(1)}, bf16[512,1536]{1,0:T(8,128)(2,1)S(1)}, u32[]{:S(2)}, u32[]{:S(2)}) collective-permute-start(bf16[512,1536]{1,0:T(8,128)(2,1)S(1)} %get-tuple-element.115), channel_id=1, source_target_pairs={{0,2},{1,3},{2,0},{3,1},{4,6},{5,7},{6,4},{7,5},{8,10},{9,11},{10,... | collective-permute-start | bytes 4718600 | tf_op jit(solution)/shard_map/ppermute | solution.py:430
  499.4 35.2 %collective-permute-start.18 = (bf16[512,1536]{1,0:T(8,128)(2,1)S(1)}, bf16[512,1536]{1,0:T(8,128)(2,1)S(1)}, u32[]{:S(2)}, u32[]{:S(2)}) collective-permute-start(bf16[512,1536]{1,0:T(8,128)(2,1)S(1)} %get-tuple-element.115), channel_id=1, source_target_pairs={{0,1},{1,0},{2,3},{3,2},{4,5},{5,4},{6,7},{7,6},{8,9},{9,8},{10,11... | collective-permute-start | bytes 4718600 | tf_op jit(solution)/shard_map/ppermute | solution.py:430
  705.3 262.3 %reduce-scatter.12.cloned.1.call-start = ((), (), s32[]{:S(2)}) async-start(), calls=%async_computation.5 | async-start | bytes 10616832
  749.3 339.4 %reduce-scatter.8.cloned.1.call-start = ((), (), s32[]{:S(2)}) async-start(), calls=%async_computation.3 | async-start | bytes 7077888 | tf_op jit(solution)/shard_map/reduce_scatter | solution.py:607
  778.9 3.5 collective-permute-start.22
  779.0 5.6 collective-permute-start.21
  783.9 36.8 %collective-permute-start.23 = (bf16[512,1536]{1,0:T(8,128)(2,1)}, bf16[512,1536]{1,0:T(8,128)(2,1)}, u32[]{:S(2)}, u32[]{:S(2)}) collective-permute-start(bf16[512,1536]{1,0:T(8,128)(2,1)} %fusion.29), channel_id=1, source_target_pairs={{0,2},{1,3},{2,0},{3,1},{4,6},{5,7},{6,4},{7,5},{8,10},{9,11},{10,... | collective-permute-start | bytes 4718600 | tf_op jit(solution)/shard_map/ppermute | solution.py:430
  826.8 3.7 collective-permute-start.27
  830.5 10.2 collective-permute-start.28
  840.7 4.5 collective-permute-start.29
  842.4 8.6 collective-permute-start.24
  845.2 5.3 collective-permute-start.30
  851.0 6.9 collective-permute-start.25
  (67 other events, 1438.7 us)
Sparse Core Ops, SparseCore 0:
  705.4 95.9 reduce-scatter.9
  805.0 162.5 reduce-scatter.11
  971.2 117.5 reduce-scatter.7

commit v2 on v1

--- a/solution.py
+++ b/solution.py
@@ -119,9 +119,10 @@
         @pl.loop(0, k_ref.shape[0] // BK)
         def _(i):
             rows = pl.ds(pl.multiple_of(i * BK, BK), BK)
-            key = turned(normed_heads(k_ref[rows, :], lane), cos_ref[rows, :], sin_ref[rows, :], lane)
+            held = pl.ds(pl.multiple_of(bounds[4, i] * BK, BK), BK)
+            key = turned(normed_heads(k_ref[held, :], lane), cos_ref[rows, :], sin_ref[rows, :], lane)
             split(kh_ref, rows, key, km_ref[rows, :].astype(f32))
-            split(vh_ref, rows, v_ref[rows, :], ones)
+            split(vh_ref, rows, v_ref[held, :], ones)
 
         @pl.loop(0, tk_ref.shape[0] // BK)
         def _(i):
@@ -281,9 +282,10 @@
         @pl.loop(0, k_ref.shape[0] // BK)
         def _(i):
             rows = pl.ds(pl.multiple_of(i * BK, BK), BK)
+            held = pl.ds(pl.multiple_of(bounds[4, i] * BK, BK), BK)
             d_key = turned_back(joined(dk_acc, rows), cos_ref[rows, :], sin_ref[rows, :], lane)
-            dk_ref[rows, :] = normed_heads_back(k_ref[rows, :], d_key, lane).astype(bf16)
-            dv_ref[rows, :] = joined(dv_acc, rows).astype(bf16)
+            dk_ref[held, :] = normed_heads_back(k_ref[held, :], d_key, lane).astype(bf16)
+            dv_ref[held, :] = joined(dv_acc, rows).astype(bf16)
 
         @pl.loop(0, tk_ref.shape[0] // BK)
         def _(i):
@@ -308,7 +310,7 @@
         num_scalar_prefetch=2,
         grid=(pairs, blocks),
         in_specs=[
-            window(BQ, lambda p, b, *_: (b, p)),
+            window(BQ, lambda p, b, at, *_: (at[4, b], p)),
             window(seq, lambda p, b, *_: (0, pairs + p)),
             window(seq, lambda p, b, *_: (0, 2 * pairs + p)),
             window(slots, lambda p, b, *_: (0, p)),
@@ -322,9 +324,9 @@
             window(slots, lambda p, b, *_: (0, 0)),
         ],
         out_specs=[
-            window(BQ, lambda p, b, *_: (b, p)),
-            window(BQ, lambda p, b, *_: (b, p)),
-            window(BQ, lambda p, b, *_: (b, p)),
+            window(BQ, lambda p, b, at, *_: (at[4, b], p)),
+            window(BQ, lambda p, b, at, *_: (at[4, b], p)),
+            window(BQ, lambda p, b, at, *_: (at[4, b], p)),
             pl.BlockSpec((2, BQ, LANES), lambda p, b, *_: (p, b, 0)),
             pl.BlockSpec((2, BQ, LANES), lambda p, b, *_: (p, b, 0)),
             per_head(seq),
@@ -364,7 +366,7 @@
     bf16, f32 = jnp.bfloat16, jnp.float32
     per_head = lambda rows: pl.BlockSpec((2, rows, LANES), lambda p, b, *_: (p, 0, 0))
     per_block = pl.BlockSpec((2, BQ, LANES), lambda p, b, *_: (p, b, 0))
-    mine = window(BQ, lambda p, b, *_: (b, p))
+    mine = window(BQ, lambda p, b, at, *_: (at[4, b], p))
     grid = pltpu.PrefetchScalarGridSpec(
         num_scalar_prefetch=2,
         grid=(pairs, blocks),
@@ -430,32 +432,34 @@
     return lax.ppermute(value, axis, [(i, i ^ bit) for i in range(size)])
 
 
-def gather_rows(mine):
-    size = lax.axis_size("mp")
-    if size != 4:
-        return lax.all_gather(mine, "mp", axis=0, tiled=True)
-    rows, me = mine.shape[0], lax.axis_index("mp")
-    across = swapped(mine, "mp", 2)
-    beside = swapped(mine, "mp", 1)
-    diagonal = swapped(across, "mp", 1)
-    out = jnp.zeros((4, rows, mine.shape[1]), mine.dtype)
-    for part, bit in ((mine, 0), (beside, 1), (across, 2), (diagonal, 3)):
-        out = lax.dynamic_update_slice(out, part[None], (me ^ bit, 0, 0))
-    return out.reshape(4 * rows, mine.shape[1])
-
-
-def scatter_rows(partial):
-    size = lax.axis_size("mp")
-    if size != 4:
-        return lax.psum_scatter(partial, "mp", scatter_dimension=0, tiled=True).astype(jnp.float32)
-    me = lax.axis_index("mp")
-    quarters = partial.reshape(4, partial.shape[0] // 4, partial.shape[1])
-    take = lambda bit: lax.dynamic_index_in_dim(quarters, me ^ bit, 0, keepdims=False)
-    far = swapped(take(3), "mp", 1)
-    near = swapped(take(1), "mp", 1)
-    summed = (take(2).astype(jnp.float32) + far.astype(jnp.float32)).astype(jnp.bfloat16)
-    other = swapped(summed, "mp", 2)
-    return take(0).astype(jnp.float32) + near.astype(jnp.float32) + other.astype(jnp.float32)
+def after(value, *others):
+    return lax.optimization_barrier((value, *others))[0]
+
+
+def near_rows(mine):
+    return jnp.concatenate([mine, swapped(mine, "mp", 1)], 0)
+
+
+def far_rows(mine, across):
+    if across is None:
+        return None
+    return jnp.concatenate([across, swapped(across, "mp", 1)], 0)
+
+
+def piece(half, at):
+    rows = half.shape[0] // 2
+    return half[at * rows : (at + 1) * rows]
+
+
+def to_across(far):
+    beside = swapped(piece(far, 1), "mp", 1)
+    return (piece(far, 0).astype(jnp.float32) + beside.astype(jnp.float32)).astype(far.dtype)
+
+
+def own_sum(near, other):
+    beside = swapped(piece(near, 1), "mp", 1)
+    total = piece(near, 0).astype(jnp.float32) + beside.astype(jnp.float32)
+    return total + other.astype(jnp.float32)
 
 
 def sum_over(value, axes):
@@ -500,6 +504,9 @@
     wide = -(-local_width // LANES) * LANES
     spare = wide - local_width
     slot_count = text_states.shape[0]
+    hidden = w_gate.shape[1]
+    halves = lax.axis_size("mp") == 4
+    turn = shard_index if halves else jnp.int32(0)
     image_ids = jnp.arange(IMGS, dtype=jnp.int32)
     token_ids = jnp.arange(seq_len, dtype=jnp.int32)
     image_ends = jnp.cumsum(image_lengths[0])
@@ -538,104 +545,191 @@
             (pick(image_ends, in_last) + BK - 1) // BK,
             in_first,
             in_last + 1,
+            (block_first // local_rows ^ turn) * (local_rows // BQ) + block_first % local_rows // BQ,
         ]
     ).astype(jnp.int32)
 
     quarter = HD // 4
     frequency = 10000.0 ** (-jnp.arange(quarter, dtype=f32) / quarter)
-    angle_row = positions[0].astype(f32)[:, None] * frequency[None, :]
-    angle_col = positions[1].astype(f32)[:, None] * frequency[None, :]
-    cos_row, sin_row, cos_col, sin_col = (
-        jnp.cos(angle_row),
-        jnp.sin(angle_row),
-        jnp.cos(angle_col),
-        jnp.sin(angle_col),
-    )
-    cos = jnp.concatenate([cos_row, cos_row, cos_col, cos_col] * 2, 1)
-    sin = jnp.concatenate([-sin_row, sin_row, -sin_col, sin_col] * 2, 1)
+    angles = (positions.astype(f32)[:, None, :] * frequency[None, :, None]).reshape(-1, seq_len)
+    lane_ids = jnp.arange(LANES, dtype=jnp.int32)
+    source = (lane_ids % HD) // (2 * quarter) * quarter + lane_ids % quarter
+    spread = (jnp.arange(2 * quarter)[:, None] == source[None, :]).astype(f32)
+    sign = jnp.where(lane_ids % (2 * quarter) < quarter, -1.0, 1.0)
+    turn_rows = (((0,), (0,)), ((), ()))
+    cos = lax.dot_general(jnp.cos(angles), spread, turn_rows, precision=highest)
+    sin = lax.dot_general(jnp.sin(angles), spread * sign[None, :], turn_rows, precision=highest)
 
     hidden_float = hidden_in.astype(f32)
     normed_one, back_norm_one = jax.vjp(modulated_norm, hidden_float, attention_gain, scale_attn)
-    rows_attn = gather_rows(normed_one.astype(bf16))
+    normed_one_low = normed_one.astype(bf16)
     tanh_ffn = jnp.tanh(gate_ffn)
     cotangent = out_cotangent.astype(f32)
-    d_ffn_all = gather_rows((cotangent * tanh_ffn).astype(bf16))
+    d_ffn_low = (cotangent * tanh_ffn).astype(bf16)
 
     widen = lambda w: jnp.pad(w, ((0, 0), (0, spare))) if spare else w
+    narrow = lambda d: d[:, :local_width] if spare else d
     w_joint = jnp.concatenate([widen(w_query), widen(w_key), widen(w_value)], 1)
     w_text = jnp.concatenate([widen(w_text_key), widen(w_text_value)], 1)
     w_out_wide = jnp.pad(w_out, ((0, spare), (0, 0))) if spare else w_out
     text_joint = jnp.dot(text_states, w_text, preferred_element_type=f32)
-    joint = jnp.dot(rows_attn, w_joint, preferred_element_type=f32)
     gate_mine = lax.dynamic_slice_in_dim(head_gates, shard_index * local_heads, local_heads, 0)
     gate_tanh = jnp.tanh(gate_mine)
     gates = jnp.pad(gate_tanh, (0, wide // HD - local_heads))
+
+    def cast_dot(left, right, numbers):
+        return lax.dot_general(left, right, numbers, preferred_element_type=f32).astype(bf16)
+
+    plain = (((1,), (0,)), ((), ()))
+
+    def feed(rows):
+        gate_pre = jnp.dot(rows, w_gate, preferred_element_type=f32)
+        up_pre = jnp.dot(rows, w_up, preferred_element_type=f32)
+        sigmoid_gate = jax.nn.sigmoid(gate_pre)
+        activated = gate_pre * sigmoid_gate
+        return gate_pre, up_pre, sigmoid_gate, activated, (activated * up_pre).astype(bf16)
+
+    def feed_back(d_rows, gate_pre, up_pre, sigmoid_gate, activated, inner_low):
+        d_inner = lax.dot_general(d_rows, w_down, contract_cols, preferred_element_type=f32)
+        d_gate_low = (
+            d_inner * up_pre * sigmoid_gate * (1.0 + gate_pre * (1.0 - sigmoid_gate))
+        ).astype(bf16)
+        d_up_low = (d_inner * activated).astype(bf16)
+        d_normed = (
+            lax.dot_general(d_gate_low, w_gate, contract_cols, preferred_element_type=f32)
+            + lax.dot_general(d_up_low, w_up, contract_cols, preferred_element_type=f32)
+        ).astype(bf16)
+        return d_gate_low, d_up_low, d_normed
+
+    def grad_of(lefts, rights):
+        return sum(
+            lax.dot_general(left, right, contract_rows, preferred_element_type=f32)
+            for left, right in zip(lefts, rights)
+        ).astype(bf16)
+
+    def sum_packs(joined):
+        return lax.psum_scatter(joined, "dp", scatter_dimension=0, tiled=True)
+
+    if halves:
+        across = swapped(normed_one_low, "mp", 2)
+        near, far = near_rows(normed_one_low), far_rows(normed_one_low, across)
+        rows_attn = jnp.concatenate([near, far], 0)
+    else:
+        rows_attn = lax.all_gather(normed_one_low, "mp", axis=0, tiled=True)
+    joint = jnp.dot(rows_attn, w_joint, preferred_element_type=f32)
+    joint, d_ffn_low = lax.optimization_barrier((joint, d_ffn_low))
+    if halves:
+        across_d = swapped(d_ffn_low, "mp", 2)
+    else:
+        d_rows = (lax.all_gather(d_ffn_low, "mp", axis=0, tiled=True),)
     mixed_low, *saved = attend(
         bounds, gates, joint, text_joint, cos, sin, query_lanes, key_lanes, text_lanes
     )
-
-    attention_out = scatter_rows(jnp.dot(mixed_low, w_out_wide, preferred_element_type=f32).astype(bf16))
+    if halves:
+        mixed_low, across_d = lax.optimization_barrier((mixed_low, across_d))
+        d_rows = (near_rows(d_ffn_low), far_rows(d_ffn_low, across_d))
+
+    def project(rows):
+        return cast_dot(rows, w_out_wide, plain)
+
+    half = seq_len // 2
+    if halves:
+        far_out = to_across(project(mixed_low[half:]))
+        attention_out = own_sum(project(mixed_low[:half]), swapped(far_out, "mp", 2))
+    else:
+        attention_out = lax.psum_scatter(
+            project(mixed_low), "mp", scatter_dimension=0, tiled=True
+        ).astype(f32)
     tanh_attn = jnp.tanh(gate_attn)
     after_attn = hidden_float + tanh_attn * attention_out
     normed_two, back_norm_two = jax.vjp(modulated_norm, after_attn, feedforward_gain, scale_ffn)
-    rows_ffn = gather_rows(normed_two.astype(bf16))
-    gate_pre = jnp.dot(rows_ffn, w_gate, preferred_element_type=f32)
-    up_pre = jnp.dot(rows_ffn, w_up, preferred_element_type=f32)
-    sigmoid_gate = jax.nn.sigmoid(gate_pre)
-    activated = gate_pre * sigmoid_gate
-    inner_low = (activated * up_pre).astype(bf16)
-    d_inner = lax.dot_general(d_ffn_all, w_down, contract_cols, preferred_element_type=f32)
-    d_gate_low = (d_inner * up_pre * sigmoid_gate * (1.0 + gate_pre * (1.0 - sigmoid_gate))).astype(
-        bf16
-    )
-    d_up_low = (d_inner * activated).astype(bf16)
-    d_normed_two = scatter_rows(
-        (
-            lax.dot_general(d_gate_low, w_gate, contract_cols, preferred_element_type=f32)
-            + lax.dot_general(d_up_low, w_up, contract_cols, preferred_element_type=f32)
-        ).astype(bf16)
-    )
-    ffn_out = scatter_rows(jnp.dot(inner_low, w_down, preferred_element_type=f32).astype(bf16))
-    block_out = (after_attn + tanh_ffn * ffn_out).astype(bf16)
-    d_gate_ffn = cotangent * ffn_out * (1.0 - tanh_ffn * tanh_ffn)
-    grad_down_t = lax.dot_general(d_ffn_all, inner_low, contract_rows, preferred_element_type=f32)
-    grad_gate = lax.dot_general(rows_ffn, d_gate_low, contract_rows, preferred_element_type=f32)
-    grad_up = lax.dot_general(rows_ffn, d_up_low, contract_rows, preferred_element_type=f32)
-
-    def sum_packs(*grads):
-        joined = jnp.concatenate([g.astype(bf16) for g in grads], 1)
-        summed = lax.psum_scatter(joined, "dp", scatter_dimension=0, tiled=True).astype(f32)
-        parts, at = [], 0
-        for g in grads:
-            parts.append(summed[:, at : at + g.shape[1]])
-            at += g.shape[1]
-        return parts
-
-    out_gate, out_up, out_down_t = sum_packs(grad_gate, grad_up, grad_down_t)
+    normed_two_low = normed_two.astype(bf16)
+    if halves:
+        across = swapped(normed_two_low, "mp", 2)
+        near = near_rows(normed_two_low)
+        fed_near = feed(near)
+        back_near = feed_back(d_rows[0], *fed_near)
+        ffn_near = cast_dot(fed_near[-1], w_down, plain)
+        across = after(across, back_near[-1], ffn_near)
+        far = far_rows(normed_two_low, across)
+        fed_far = feed(far)
+        back_far = feed_back(d_rows[1], *fed_far)
+        rows_ffn, inner, d_gate, d_up = (
+            (near, far),
+            (fed_near[-1], fed_far[-1]),
+            (back_near[0], back_far[0]),
+            (back_near[1], back_far[1]),
+        )
+        other = swapped(to_across(back_far[-1]), "mp", 2)
+        ffn_far = cast_dot(after(fed_far[-1], back_far[-1]), w_down, plain)
+    else:
+        rows_ffn = (lax.all_gather(normed_two_low, "mp", axis=0, tiled=True),)
+        fed = feed(rows_ffn[0])
+        back = feed_back(d_rows[0], *fed)
+        inner, d_gate, d_up = (fed[-1],), (back[0],), (back[1],)
+        d_normed_two = lax.psum_scatter(back[-1], "mp", scatter_dimension=0, tiled=True).astype(f32)
+        ffn_out = lax.psum_scatter(
+            cast_dot(fed[-1], w_down, plain), "mp", scatter_dimension=0, tiled=True
+        ).astype(f32)
+    joined_ffn = jnp.concatenate(
+        [grad_of(rows_ffn, d_gate), grad_of(rows_ffn, d_up), grad_of(d_rows, inner)], 1
+    )
+    if halves:
+        other, joined_ffn, ffn_far = lax.optimization_barrier((other, joined_ffn, ffn_far))
+        d_normed_two = own_sum(back_near[-1], other)
+    out_ffn = sum_packs(joined_ffn)
 
     d_after_norm, grad_ffn_gain, d_scale_ffn = back_norm_two(d_normed_two)
     d_after = cotangent + d_after_norm
     d_attn_low = (d_after * tanh_attn).astype(bf16)
     d_gate_attn = d_after * attention_out * (1.0 - tanh_attn * tanh_attn)
-    d_attn_all = gather_rows(d_attn_low)
-    grad_out_t = lax.dot_general(d_attn_all, mixed_low, contract_rows, preferred_element_type=f32)
+    if halves:
+        across = swapped(d_attn_low, "mp", 2)
+        d_attn_all = jnp.concatenate([near_rows(d_attn_low), far_rows(d_attn_low, across)], 0)
+    else:
+        d_attn_all = lax.all_gather(d_attn_low, "mp", axis=0, tiled=True)
     d_mixed = lax.dot_general(d_attn_all, w_out_wide, contract_cols, preferred_element_type=f32)
+    if halves:
+        other = swapped(to_across(after(ffn_far, d_mixed)), "mp", 2)
     d_query, d_key, d_value, d_text_key, d_text_value, d_heads = attend_back(
         bounds, gates, d_mixed, saved, joint, text_joint, cos, sin
     )
+    if halves:
+        d_text_key, other = lax.optimization_barrier((d_text_key, other))
+        ffn_out = own_sum(ffn_near, other)
+    block_out = (after_attn + tanh_ffn * ffn_out).astype(bf16)
+    d_gate_ffn = cotangent * ffn_out * (1.0 - tanh_ffn * tanh_ffn)
     grad_heads = jnp.sum(d_heads, 1).reshape(wide // HD, HD).sum(1)[:local_heads]
     grad_heads = grad_heads * (1.0 - gate_tanh * gate_tanh)
-    narrow = lambda d: d[:, :local_width]
     d_text_low = jnp.concatenate([narrow(d_text_key), narrow(d_text_value)], 1)
-    grad_text = lax.dot_general(text_states, d_text_low, contract_rows, preferred_element_type=f32)
-    (out_text,) = sum_packs(grad_text)
-    d_joint_low = jnp.concatenate([d_query, d_key, d_value], 1)
-    d_normed_one = scatter_rows(
-        lax.dot_general(d_joint_low, w_joint, contract_cols, preferred_element_type=f32).astype(bf16)
-    )
-    d_joint_low = jnp.concatenate([narrow(d_query), narrow(d_key), narrow(d_value)], 1)
-    grad_joint = lax.dot_general(rows_attn, d_joint_low, contract_rows, preferred_element_type=f32)
-    out_joint, out_out_t = sum_packs(grad_joint, narrow(grad_out_t))
+    joined_text = grad_of((text_states,), (d_text_low,))
+    joined_text, out_ffn = lax.optimization_barrier((joined_text, out_ffn))
+    out_text = sum_packs(joined_text)
+    d_joint_low = after(jnp.concatenate([d_query, d_key, d_value], 1), joined_text)
+    d_rows_one = lambda d: cast_dot(d, w_joint, contract_cols)
+    if halves:
+        other = swapped(to_across(d_rows_one(d_joint_low[half:])), "mp", 2)
+        near_one = d_rows_one(d_joint_low[:half])
+    else:
+        d_normed_one = lax.psum_scatter(
+            d_rows_one(d_joint_low), "mp", scatter_dimension=0, tiled=True
+        ).astype(f32)
+    joined_attn = jnp.concatenate(
+        [
+            grad_of((rows_attn,), (narrow(d_query),)),
+            grad_of((rows_attn,), (narrow(d_key),)),
+            grad_of((rows_attn,), (narrow(d_value),)),
+            grad_of((d_attn_all,), (narrow(mixed_low),)),
+        ],
+        1,
+    ) if spare else jnp.concatenate(
+        [grad_of((rows_attn,), (d_joint_low,)), grad_of((d_attn_all,), (mixed_low,))], 1
+    )
+    if halves:
+        other, joined_attn = lax.optimization_barrier((other, joined_attn))
+        d_normed_one = own_sum(near_one, other)
+    out_attn = sum_packs(joined_attn)
+    out_attn, out_text, out_ffn = (out.astype(f32) for out in (out_attn, out_text, out_ffn))
 
     d_hidden_norm, grad_attn_gain, d_scale_attn = back_norm_one(d_normed_one)
     input_grad = (d_after + d_hidden_norm).astype(bf16)
@@ -651,15 +745,15 @@
         block_out,
         input_grad,
         modulation_grad,
-        out_joint[:, 0:local_width],
-        out_joint[:, local_width : 2 * local_width],
-        out_joint[:, 2 * local_width :],
-        out_out_t.T,
+        out_attn[:, 0:local_width],
+        out_attn[:, local_width : 2 * local_width],
+        out_attn[:, 2 * local_width : 3 * local_width],
+        out_attn[:, 3 * local_width :].T,
         out_text[:, 0:local_width],
         out_text[:, local_width:],
-        out_gate,
-        out_up,
-        out_down_t.T,
+        out_ffn[:, 0:hidden],
+        out_ffn[:, hidden : 2 * hidden],
+        out_ffn[:, 2 * hidden :].T,
         small[0:D],
         small[D : 2 * D],
         small[2 * D :],

time: 1110 us -> 891 us (0.80)
  waiting for transfers between devices: 453 us -> 256 us
  local copies, waits for them, and re-layouts: 115 us -> 69.5 us
  matrix products: 189 us -> 207 us
    reduce_scatter x1, waiting for transfers between devices: 108 us -> 0.01 us  [sum_packs(): return lax.psum_scatter(joined, 'dp', scatter_dimension=0, tiled=True)]
    ppermute x31, waiting for transfers between devices: 241 us -> 164 us  [swapped(): return lax.ppermute(value, axis, [(i, i ^ bit) for i in range(size)])]
    unnamed x148 -> x178, local copies, waits for them, and re-layouts: 64.7 us -> 48.6 us
    concatenate x3, local copies, waits for them, and re-layouts: 16.1 us -> 0.31 us  [the longest x2 0.21 us: far_rows(): return jnp.concatenate([across, swapped(across, 'mp', 1)], 0)]
    dot_general x14 -> x27, matrix products: 142 us -> 157 us  [the longest x9 62.2 us: grad_of(): lax.dot_general(left, right, contract_rows, preferred_element_type=f32)]
    dynamic_update_slice x12 -> x0, local copies, waits for them, and re-layouts: 12.2 us -> none  [gather_rows(): out = lax.dynamic_update_slice(out, part[None], (me ^ bit, 0, 0))]
    unnamed x5, waiting for transfers between devices: 104 us -> 92.7 us
  transfers between devices with their start and end apart: 34 -> 34, of which waited for: 18 -> 16; matrix products, arithmetic and copies ran while one was open for 18% -> 26% of each run, Pallas kernels for 0% -> 29%
where the time goes in v2:
time: 891 us; the launch traced here: 883 us
  waiting for transfers between devices  256 us (29%)
  Pallas kernels  256 us (29%)
  matrix products  207 us (23%)
  local copies, waits for them, and re-layouts  69.5 us (8%)
  other arithmetic  61 us (7%)
  starting transfers between devices  18.6 us (2%)
  between operations  15.1 us (2%)
    ppermute x31, waiting for transfers between devices, swapped(): return lax.ppermute(value, axis, [(i, i ^ bit) for i in range(size)])  164 us
    pallas_call x1, Pallas kernels, attend_back(): pl.pallas_call(attend_back_kernel, grid_spec=grid, out_shape=[jax.ShapeDt...  136 us
    pallas_call x1, Pallas kernels, attend(): pl.pallas_call(attend_kernel, grid_spec=grid, out_shape=[jax.ShapeDtypeSt...  120 us
    unnamed x5, waiting for transfers between devices  92.7 us
    dot_general x9, matrix products, grad_of(): lax.dot_general(left, right, contract_rows, preferred_element_type=f32)  62.2 us
    unnamed x178, local copies, waits for them, and re-layouts  48.6 us
    dot_general x6, matrix products, cast_dot(): lax.dot_general(left, right, numbers, preferred_element_type=f32)  26.5 us
    ppermute x31, starting transfers between devices, swapped(): return lax.ppermute(value, axis, [(i, i ^ bit) for i in range(size)])  18.5 us
  transfers between devices with their start and end apart: 34, of which 16 were waited for; matrix products, arithmetic and copies ran while one was open for 26% of the time, Pallas kernels for 29%

profile of v2, /device:TPU:0, one launch (start us, length us, event | category | flops | bytes accessed | tf_op | source)
XLA Modules:
  0.0 883.3 jit_solution(14783102985068182459)
XLA Ops:
  12.0 6.1 fusion.51
  45.4 16.0 %collective-permute-done.1 = bf16[512,1536]{1,0:T(8,128)(2,1)} collective-permute-done((bf16[512,1536]{1,0:T(8,128)(2,1)}, bf16[512,1536]{1,0:T(8,128)(2,1)}, u32[]{:S(2)}, u32[]{:S(2)}) %collective-permute-start.1) | collective-permute-done | bytes 1572896 | tf_op jit(solution)/shard_map/ppermute | solution.py:432
  61.3 12.3 %fusion.15.tk_ref.tv_ref = f32[1280,768]{1,0:T(8,128)} fusion(bf16[1280,4096]{1,0:T(8,128)(2,1)} %param.20, bf16[4096,384]{1,0:T(8,128)(2,1)S(1)} %copy-done.50, bf16[4096,384]{1,0:T(8,128)(2,1)S(1)} %copy-done.51), kind=kOutput, calls=%fused_computation.45 | convolution fusion | flops 8065646592 | bytes 20709376 | tf_op jit(solution)/shard_map/dot_general | solution.py:575
  73.7 15.9 %fusion.37.q_ref.k_ref.v_ref = f32[2048,1152]{1,0:T(8,128)} fusion(bf16[1536,1152]{1,0:T(8,128)(2,1)S(1)} %constant_dynamic-update-slice_fusion, bf16[512,1536]{1,0:T(8,128)(2,1)S(1)} %collective-permute-done.2, bf16[512,1536]{1,0:T(8,128)(2,1)} %collective-permute-done.1, bf16[512,1536]{1,0:T(8,128)(2,1)} %collective-permute-done, ...), kind=kOutput, calls=%fused_computation.97 | convolution fusion | flops 7272923136 | bytes 19267584 | tf_op jit(solution)/shard_map/dot_general | solution.py:619
  91.3 119.9 %attend.1 = (bf16[2048,384]{1,0:T(8,128)(2,1)}, f32[2048,384]{1,0:T(8,128)}, f32[2048,384]{1,0:T(8,128)}, bf16[6,2048,128]{2,1,0:T(8,128)(2,1)}, bf16[6,2048,128...) custom-call(s32[5,8]{1,0:T(8,128)} %stack.5.bounds, ...), custom_call_target="tpu_custom_call" | custom-call | flops 20000000000 | bytes 30000000 | tf_op jit(solution)/shard_map/attend/pallas_call | solution.py:340
  220.6 34.8 %collective-permute-done.6 = bf16[512,1536]{1,0:T(8,128)(2,1)S(1)} collective-permute-done((bf16[512,1536]{1,0:T(8,128)(2,1)S(1)}, bf16[512,1536]{1,0:T(8,128)(2,1)S(1)}, u32[]{:S(2)}, u32[]{:S(2)}) %collective-permute-start.6) | collective-permute-done | bytes 1572896 | tf_op jit(solution)/shard_map/ppermute | solution.py:432
  264.7 5.8 fusion.85
  270.5 9.4 %multiply_convert_fusion.5 = (bf16[1024,1024]{1,0:T(8,128)(2,1)}, bf16[1024,1024]{1,0:T(8,128)(2,1)}, bf16[1024,1024]{1,0:T(8,128)(2,1)}) fusion(f32[1024,1024]{1,0:T(8,128)} %fusion.85, f32[1024,1024]{1,0:T(8,128)S(1)} %fusion.92, bf16[1536,1024]{1,0:T(8,128)(2,1)S(1)} %copy-done, bf16[512,1536]{1,0:T(8,128)(2,1)S(1)} %collective-permute-done.7, ...), kind=kOutput, calls=%fused_computation.42 | convolution fusion | flops 3243245568 | bytes 20971520 | tf_op jit(solution)/shard_map/dot_general | solution.py:587
  280.0 7.1 fusion.93
  291.9 6.9 add_convert_fusion.4
  311.1 7.6 multiply_convert_fusion
  318.7 7.2 fusion.96
  331.4 5.5 fusion.98
  336.9 5.6 add_convert_fusion.3
  344.0 5.7 add_convert_fusion.1
  349.7 6.5 add_convert_fusion.2
  356.3 5.7 fusion.99
  361.9 5.8 add_convert_fusion
  378.8 26.3 %collective-permute-done.15 = bf16[512,1536]{1,0:T(8,128)(2,1)} collective-permute-done((bf16[512,1536]{1,0:T(8,128)(2,1)S(1)}, bf16[512,1536]{1,0:T(8,128)(2,1)}, u32[]{:S(2)}, u32[]{:S(2)}) %collective-permute-start.15) | collective-permute-done | bytes 1572896 | tf_op jit(solution)/shard_map/ppermute | solution.py:432
  405.1 12.7 %copy.80 = bf16[1536,3072]{1,0:T(8,128)(2,1)} copy(bf16[1536,3072]{0,1:T(8,128)(2,1)} %pad_maximum_fusion) | data formatting | bytes 18874368
  423.1 6.3 multiply_reduce_fusion
  438.1 36.1 %collective-permute-done.17 = bf16[512,1536]{1,0:T(8,128)(2,1)S(1)} collective-permute-done((bf16[512,1536]{1,0:T(8,128)(2,1)S(1)}, bf16[512,1536]{1,0:T(8,128)(2,1)S(1)}, u32[]{:S(2)}, u32[]{:S(2)}) %collective-permute-start.17) | collective-permute-done | bytes 1572896 | tf_op jit(solution)/shard_map/ppermute | solution.py:432
  477.6 8.4 fusion.38.dm_ref
  491.5 135.9 %attend_back.1 = (bf16[2048,384]{1,0:T(8,128)(2,1)}, bf16[2048,384]{1,0:T(8,128)(2,1)}, bf16[2048,384]{1,0:T(8,128)(2,1)}, bf16[1280,384]{1,0:T(8,128)(2,1)}, bf...) custom-call(s32[5,8]{1,0:T(8,128)} %stack.5.bounds, f32[6]{0:T(128)} %dynamic-slice_tanh_fusion.gates, ...), custom_call_target="tpu_custom_call" | custom-call | flops 60000002048 | bytes 40000000 | tf_op jit(solution)/shard_map/attend_back/pallas_call | solution.py:409
  627.4 13.7 %fusion.12 = bf16[4096,768]{0,1:T(8,128)(2,1)} fusion(bf16[1280,4096]{1,0:T(8,128)(2,1)} %param.20, bf16[1280,384]{1,0:T(8,128)(2,1)} %get-tuple-element.71, bf16[1280,384]{1,0:T(8,128)(2,1)} %get-tuple-element.70), kind=kOutput, calls=%fused_computation.27 | convolution fusion | flops 8060141568 | bytes 18743296 | tf_op jit(solution)/shard_map/dot_general | solution.py:606
  658.6 9.7 %convolution_convert_fusion = bf16[1536,1152]{0,1:T(8,128)(2,1)S(1)} fusion(bf16[2048,1152]{1,0:T(8,128)(2,1)S(1)} %pad_maximum_fusion.3, bf16[512,1536]{1,0:T(8,128)(2,1)S(1)} %copy-done.57, bf16[512,1536]{1,0:T(8,128)(2,1)} %collective-permute-done.1, bf16[512,1536]{1,0:T(8,128)(2,1)} %collective-permute-done, bf16[512,1536]{1,0:T(8,128)(2,1)} %get-tuple-element.157), kind=kOutput, calls=%fused_computation.9 | convolution fusion | flops 7274692608 | bytes 14548992 | tf_op jit(solution)/shard_map/dot_general | solution.py:606
  670.7 22.8 %collective-permute-done.23 = bf16[512,1536]{1,0:T(8,128)(2,1)} collective-permute-done((bf16[512,1536]{1,0:T(8,128)(2,1)S(1)}, bf16[512,1536]{1,0:T(8,128)(2,1)}, u32[]{:S(2)}, u32[]{:S(2)}) %collective-permute-start.23) | collective-permute-done | bytes 1572896 | tf_op jit(solution)/shard_map/ppermute | solution.py:432
  693.5 6.6 copy.82
  702.8 7.1 convolution_convert_fusion.7
  716.8 11.6 %fusion.25 = (f32[512,1536]{1,0:T(8,128)}, bf16[512,1536]{1,0:T(8,128)(2,1)}, f32[512]{0:T(512)S(1)}, f32[1536]{0:T(1024)S(1)}, f32[512,1536]{1,0:T(8,128)}, /*index=5*/f32[512,1536]{1,0:T(8,128)}) fusion(bf16[512,1536]{1,0:T(8,128)(2,1)} %param.37, f32[512,6144]{1,0:T(8,128)} %copy-done.2, bf16[512,1536]{1,0:T(8,128)(2,1)} %collective-permute-done.20, ...), kind=kLoop, calls=%fused_computation.59 | loop fusion | flops 22804480 | bytes 33046528 | tf_op jit(solution)/shard_map/mul | solution.py:701
  741.2 7.3 fusion
  770.6 92.6 %reduce-scatter.12.cloned.1.call-done = bf16[192,1536]{1,0:T(8,128)(2,1)} async-done(((bf16[1536,1536]{1,0:T(8,128)(2,1)}), bf16[192,1536]{1,0:T(8,128)(2,1)}) %reduce-scatter.12.cloned.1.call-update) | async-done | bytes 589840
  (334 shorter events, 187.2 us)
Async XLA Ops:
  7.2 633.9 %reduce-scatter.10.cloned.1.call-start = ((), (), s32[]{:S(2)}) async-start(), calls=%async_computation.4 | async-start | bytes 10616832
  23.7 37.7 %collective-permute-start.1 = (bf16[512,1536]{1,0:T(8,128)(2,1)}, bf16[512,1536]{1,0:T(8,128)(2,1)}, u32[]{:S(2)}, u32[]{:S(2)}) collective-permute-start(bf16[512,1536]{1,0:T(8,128)(2,1)} %get-tuple-element.157), channel_id=1, source_target_pairs={{0,2},{1,3},{2,0},{3,1},{4,6},{5,7},{6,4},{7,5},{8,10},{9,11},{10,... | collective-permute-start | bytes 4718600 | tf_op jit(solution)/shard_map/ppermute | solution.py:432
  26.6 47.1 %collective-permute-start = (bf16[512,1536]{1,0:T(8,128)(2,1)}, bf16[512,1536]{1,0:T(8,128)(2,1)}, u32[]{:S(2)}, u32[]{:S(2)}) collective-permute-start(bf16[512,1536]{1,0:T(8,128)(2,1)} %get-tuple-element.157), channel_id=1, source_target_pairs={{0,1},{1,0},{2,3},{3,2},{4,5},{5,4},{6,7},{7,6},{8,9},{9,8},{10,11... | collective-permute-start | bytes 4718600 | tf_op jit(solution)/shard_map/ppermute | solution.py:432
  61.3 12.4 %collective-permute-start.2 = (bf16[512,1536]{1,0:T(8,128)(2,1)}, bf16[512,1536]{1,0:T(8,128)(2,1)S(1)}, u32[]{:S(2)}, u32[]{:S(2)}) collective-permute-start(bf16[512,1536]{1,0:T(8,128)(2,1)} %collective-permute-done.1), channel_id=1, source_target_pairs={{0,1},{1,0},{2,3},{3,2},{4,5},{5,4},{6,7},{7,6},{8,9},{9,8},{10,11... | collective-permute-start | bytes 4718600 | tf_op jit(solution)/shard_map/ppermute | solution.py:432
  89.6 121.7 %collective-permute-start.3 = (bf16[512,1536]{1,0:T(8,128)(2,1)}, bf16[512,1536]{1,0:T(8,128)(2,1)}, u32[]{:S(2)}, u32[]{:S(2)}) collective-permute-start(bf16[512,1536]{1,0:T(8,128)(2,1)} %get-tuple-element.49), channel_id=1, source_target_pairs={{0,2},{1,3},{2,0},{3,1},{4,6},{5,7},{6,4},{7,5},{8,10},{9,11},{10,... | collective-permute-start | bytes 4718600 | tf_op jit(solution)/shard_map/ppermute | solution.py:432
  214.9 3.5 collective-permute-start.5
  217.1 3.5 collective-permute-start.4
  218.8 36.6 %collective-permute-start.6 = (bf16[512,1536]{1,0:T(8,128)(2,1)S(1)}, bf16[512,1536]{1,0:T(8,128)(2,1)S(1)}, u32[]{:S(2)}, u32[]{:S(2)}) collective-permute-start(bf16[512,1536]{1,0:T(8,128)(2,1)S(1)} %add_convert_fusion.9), channel_id=1, source_target_pairs={{0,2},{1,3},{2,0},{3,1},{4,6},{5,7},{6,4},{7,5},{8,10},{9,11},{10,... | collective-permute-start | bytes 4718600 | tf_op jit(solution)/shard_map/ppermute | solution.py:432
  219.1 41.5 %collective-permute-start.9 = (bf16[512,1536]{1,0:T(8,128)(2,1)}, bf16[512,1536]{1,0:T(8,128)(2,1)S(1)}, u32[]{:S(2)}, u32[]{:S(2)}) collective-permute-start(bf16[512,1536]{1,0:T(8,128)(2,1)} %get-tuple-element.49), channel_id=1, source_target_pairs={{0,1},{1,0},{2,3},{3,2},{4,5},{5,4},{6,7},{7,6},{8,9},{9,8},{10,11... | collective-permute-start | bytes 4718600 | tf_op jit(solution)/shard_map/ppermute | solution.py:432
  258.6 6.2 collective-permute-start.7
  260.2 42.0 %collective-permute-start.11 = (bf16[512,1536]{1,0:T(8,128)(2,1)}, bf16[512,1536]{1,0:T(8,128)(2,1)S(1)}, u32[]{:S(2)}, u32[]{:S(2)}) collective-permute-start(bf16[512,1536]{1,0:T(8,128)(2,1)} %collective-permute-done.3), channel_id=1, source_target_pairs={{0,1},{1,0},{2,3},{3,2},{4,5},{5,4},{6,7},{7,6},{8,9},{9,8},{10,11... | collective-permute-start | bytes 4718600 | tf_op jit(solution)/shard_map/ppermute | solution.py:432
  264.4 36.4 %collective-permute-start.12 = (bf16[512,1536]{1,0:T(8,128)(2,1)S(1)}, bf16[512,1536]{1,0:T(8,128)(2,1)S(1)}, u32[]{:S(2)}, u32[]{:S(2)}) collective-permute-start(bf16[512,1536]{1,0:T(8,128)(2,1)S(1)} %multiply_convert_fusion.7), channel_id=1, source_target_pairs={{0,2},{1,3},{2,0},{3,1},{4,6},{5,7},{6,4},{7,5},{8,10},{9,11},{10,... | collective-permute-start | bytes 4718600 | tf_op jit(solution)/shard_map/ppermute | solution.py:432
  300.7 6.8 collective-permute-start.13
  342.6 25.2 %collective-permute-start.14 = (bf16[512,1536]{1,0:T(8,128)(2,1)S(1)}, bf16[512,1536]{1,0:T(8,128)(2,1)S(1)}, u32[]{:S(2)}, u32[]{:S(2)}) collective-permute-start(bf16[512,1536]{1,0:T(8,128)(2,1)S(1)} %slice.157), channel_id=1, source_target_pairs={{0,1},{1,0},{2,3},{3,2},{4,5},{5,4},{6,7},{7,6},{8,9},{9,8},{10,11... | collective-permute-start | bytes 4718600 | tf_op jit(solution)/shard_map/ppermute | solution.py:432
  368.1 37.0 %collective-permute-start.15 = (bf16[512,1536]{1,0:T(8,128)(2,1)S(1)}, bf16[512,1536]{1,0:T(8,128)(2,1)}, u32[]{:S(2)}, u32[]{:S(2)}) collective-permute-start(bf16[512,1536]{1,0:T(8,128)(2,1)S(1)} %add_convert_fusion.8), channel_id=1, source_target_pairs={{0,2},{1,3},{2,0},{3,1},{4,6},{5,7},{6,4},{7,5},{8,10},{9,11},{10,... | collective-permute-start | bytes 4718600 | tf_op jit(solution)/shard_map/ppermute | solution.py:432
  417.9 349.1 %reduce-scatter.8.cloned.1.call-start = ((), (), s32[]{:S(2)}) async-start(), calls=%async_computation.3 | async-start | bytes 7077888 | tf_op jit(solution)/shard_map/reduce_scatter | solution.py:611
  419.6 3.5 collective-permute-start.10
  437.9 36.3 %collective-permute-start.17 = (bf16[512,1536]{1,0:T(8,128)(2,1)S(1)}, bf16[512,1536]{1,0:T(8,128)(2,1)S(1)}, u32[]{:S(2)}, u32[]{:S(2)}) collective-permute-start(bf16[512,1536]{1,0:T(8,128)(2,1)S(1)} %multiply_convert_fusion.6), channel_id=1, source_target_pairs={{0,2},{1,3},{2,0},{3,1},{4,6},{5,7},{6,4},{7,5},{8,10},{9,11},{10,... | collective-permute-start | bytes 4718600 | tf_op jit(solution)/shard_map/ppermute | solution.py:432
  438.1 36.2 %collective-permute-start.16 = (bf16[512,1536]{1,0:T(8,128)(2,1)S(1)}, bf16[512,1536]{1,0:T(8,128)(2,1)S(1)}, u32[]{:S(2)}, u32[]{:S(2)}) collective-permute-start(bf16[512,1536]{1,0:T(8,128)(2,1)S(1)} %multiply_convert_fusion.6), channel_id=1, source_target_pairs={{0,1},{1,0},{2,3},{3,2},{4,5},{5,4},{6,7},{7,6},{8,9},{9,8},{10,11... | collective-permute-start | bytes 4718600 | tf_op jit(solution)/shard_map/ppermute | solution.py:432
  486.2 3.5 collective-permute-start.19
  491.2 136.2 %collective-permute-start.20 = (bf16[512,1536]{1,0:T(8,128)(2,1)}, bf16[512,1536]{1,0:T(8,128)(2,1)}, u32[]{:S(2)}, u32[]{:S(2)}) collective-permute-start(bf16[512,1536]{1,0:T(8,128)(2,1)} %add_convert_fusion.7), channel_id=1, source_target_pairs={{0,2},{1,3},{2,0},{3,1},{4,6},{5,7},{6,4},{7,5},{8,10},{9,11},{10,... | collective-permute-start | bytes 4718600 | tf_op jit(solution)/shard_map/ppermute | solution.py:432
  643.7 219.5 %reduce-scatter.12.cloned.1.call-start = ((), (), s32[]{:S(2)}) async-start(), calls=%async_computation.5 | async-start | bytes 5308416
  651.8 4.5 collective-permute-start.22
  656.8 36.7 %collective-permute-start.23 = (bf16[512,1536]{1,0:T(8,128)(2,1)S(1)}, bf16[512,1536]{1,0:T(8,128)(2,1)}, u32[]{:S(2)}, u32[]{:S(2)}) collective-permute-start(bf16[512,1536]{1,0:T(8,128)(2,1)S(1)} %add_convert_fusion.5), channel_id=1, source_target_pairs={{0,2},{1,3},{2,0},{3,1},{4,6},{5,7},{6,4},{7,5},{8,10},{9,11},{10,... | collective-permute-start | bytes 4718600 | tf_op jit(solution)/shard_map/ppermute | solution.py:432
  702.8 11.0 %collective-permute-start.8 = (bf16[512,1536]{1,0:T(8,128)(2,1)}, bf16[512,1536]{1,0:T(8,128)(2,1)}, u32[]{:S(2)}, u32[]{:S(2)}) collective-permute-start(bf16[512,1536]{1,0:T(8,128)(2,1)} %slice.153), channel_id=1, source_target_pairs={{0,1},{1,0},{2,3},{3,2},{4,5},{5,4},{6,7},{7,6},{8,9},{9,8},{10,11... | collective-permute-start | bytes 4718600 | tf_op jit(solution)/shard_map/ppermute | solution.py:432
  712.9 3.9 collective-permute-start.21
  730.6 9.1 %collective-permute-start.27 = (f32[3096]{0:T(1024)S(1)}, f32[3096]{0:T(1024)S(1)}, u32[]{:S(2)}, u32[]{:S(2)}) collective-permute-start(f32[3096]{0:T(1024)S(1)} %fusion.144), channel_id=1, source_target_pairs={{0,2},{1,3},{2,0},{3,1},{4,6},{5,7},{6,4},{7,5},{8,10},{9,11},{10,... | collective-permute-start | bytes 37160 | tf_op jit(solution)/shard_map/ppermute | solution.py:432
  739.8 8.8 collective-permute-start.28
  748.6 5.5 collective-permute-start.29
  750.9 9.5 %collective-permute-start.24 = (f32[5,6144]{1,0:T(8,128)S(1)}, f32[5,6144]{1,0:T(8,128)S(1)}, u32[]{:S(2)}, u32[]{:S(2)}) collective-permute-start(f32[5,6144]{1,0:T(8,128)S(1)} %fusion), channel_id=1, source_target_pairs={{0,1},{1,0},{2,3},{3,2},{4,5},{5,4},{6,7},{7,6},{8,9},{9,8},{10,11... | collective-permute-start | bytes 368648 | tf_op jit(solution)/shard_map/ppermute | solution.py:432
  754.0 5.9 collective-permute-start.30
  760.5 5.7 collective-permute-start.25
  (82 other events, 1193.6 us)
Sparse Core Ops, SparseCore 0:
  418.0 162.6 reduce-scatter.9
  643.8 120.7 reduce-scatter.7
  768.3 94.9 reduce-scatter.11
